TPU v7x, 32 devices: a whole 2x2x4 slice. The times are simulated.
32 devices in a mesh: grid: 8 (over z, y), dom: 4 (over x, core).
Axes of the slice: x: 2, y: 2, z: 4, core: 2. Of those that a mesh axis runs over, the one named last changes fastest.
Arguments:
- fields: float32 [8, 16, 16, 16, 256], P('grid', 'dom'), may hold values from -6 to 6
- cutoffs: int32 [8, 4], P('grid'), may hold values from 0 to 2
- weights: int32 [8], P('grid'), may hold values from -3 to 3, as said below
- diffusion: float32 [4], replicated, may hold values from 0.03 to 0.12
- courant: float32 [4], replicated, may hold values from -0.2 to 0.2
Outputs:
- combined_fields: float32 [8, 16, 16, 16, 256], P('grid', 'dom')
Inputs may be any that keep to these rules, and one draw needn't show every extreme that they name: `weights`: each weight is a nonzero integer of magnitude 1 to 3.
All inputs are finite; a program needn't handle non-finite values.
Results may differ from a plain program's by a relative error of at most 0.0003.
Values sent between devices are 32-bit elements; how exact they have to be, the bound alone decides.
No kernel may reach another device: no remote copies, remote signals or barrier semaphores. Data moves between devices by JAX's collectives and lax.ppermute only.
A program may use at most 64 MiB of HBM per device.

v0:
```python
import functools

import jax
import jax.numpy as jnp
from jax import lax
from jax.experimental import pallas as pl
from jax.experimental.pallas import tpu as pltpu
from jax.sharding import PartitionSpec as P


STEPS = 2
HALO = 8
TILE = 8
LANES = 128
GROUP = 16
EAGER = "ab"
CHAINS = 2

VMEM = pl.BlockSpec(memory_space=pltpu.VMEM)
SMEM = pl.BlockSpec(memory_space=pltpu.SMEM)
FAR = pl.BlockSpec(memory_space=pltpu.HBM)


def params(*arrays):
    held = sum(a.size * a.dtype.itemsize for a in arrays)
    return pltpu.CompilerParams(vmem_limit_bytes=min(2 * held + (4 << 20), 60 << 20))


def floats(*shape):
    return jax.ShapeDtypeStruct(shape, jnp.float32)


def swapped(x, axis, bit):
    size = lax.axis_size(axis)
    return lax.ppermute(x, axis, [(i, i ^ bit) for i in range(size)])


def turned(i, core, count):
    return (i + core) % count


def swapped_in_turn(x, i, count):
    grids, dom = lax.axis_size("grid"), lax.axis_size("dom")
    pairs = []
    for g in range(grids):
        for d in range(dom):
            pairs.append((g * dom + d, (g ^ 1 << turned(i, d & 1, count)) * dom + d))
    return lax.ppermute(x, ("grid", "dom"), pairs)


def halves(x):
    high = x.astype(jnp.bfloat16)
    return high, (x - high.astype(jnp.float32)).astype(jnp.bfloat16)


def split_product(x, m_high, m_low=None):
    high, low = halves(x)
    dot = functools.partial(jnp.dot, preferred_element_type=jnp.float32)
    total = dot(high, m_high) + dot(low, m_high)
    return total if m_low is None else total + dot(high, m_low)


def divides(place, cutoff):
    return (jnp.bitwise_and(place, jnp.left_shift(1, cutoff) - 1) == 0).astype(jnp.float32)


def piece_at(slot, count):
    place, core = lax.axis_index("grid"), jnp.bitwise_and(lax.axis_index("dom"), 1)
    piece = jnp.bitwise_and(place, (1 << count) - 1)
    for i in range(count):
        if slot >> i & 1:
            piece = piece ^ jnp.left_shift(1, lax.rem(i + core, count))
    return piece


def surplus_entry(source, target, length):
    low = jnp.bitwise_and(target, 3)
    hop = jnp.where(low == 0, 0, jnp.where(low == 2, 2, 1))
    gap = jnp.bitwise_and(source - target, length - 1)
    beside = (gap == hop).astype(jnp.float32) + (gap == jnp.bitwise_and(-hop, length - 1)).astype(jnp.float32)
    return (gap == 0).astype(jnp.float32) - jnp.where(hop > 0, 0.5, 0.0) * beside


def restore_entry(source, target, length):
    low = jnp.bitwise_and(target, 3)
    gap = jnp.bitwise_and(source - target, length - 1)

    def at(by):
        return (gap == by % length).astype(jnp.float32)

    one = 0.75 * at(-1) + 0.5 * at(1) + 0.25 * at(3)
    three = 0.75 * at(1) + 0.5 * at(-1) + 0.25 * at(-3)
    two = 0.5 * (at(-2) + at(2))
    beside = jnp.where(low == 0, 0.0, jnp.where(low == 2, two, jnp.where(low == 1, one, three)))
    return at(0) + beside


def tables_kernel(lens, cut_ref, weight_ref, diff_ref, cour_ref, rate_high, rate_low, surplus_ref, restore_ref):
    second_len, third_len = lens
    shape = surplus_ref.shape
    row, col = (lax.broadcasted_iota(jnp.int32, shape, d) for d in (0, 1))
    shift = third_len.bit_length() - 1
    s_row, s_col = jnp.right_shift(row, shift), jnp.right_shift(col, shift)
    t_row, t_col = jnp.bitwise_and(row, third_len - 1), jnp.bitwise_and(col, third_len - 1)
    s_gap = jnp.bitwise_and(s_row - s_col, second_len - 1)
    t_gap = jnp.bitwise_and(t_row - t_col, third_len - 1)

    def where(cond, value):
        return jnp.where(cond, value, 0.0)

    spread = diff_ref[0] + diff_ref[1] + diff_ref[2] + diff_ref[3]
    rate = where((s_gap == 0) & (t_gap == 0), -2.0 * spread)
    rate += where((s_gap == 1) & (t_gap == 0), diff_ref[1] - cour_ref[1])
    rate += where((s_gap == second_len - 1) & (t_gap == 0), diff_ref[1] + cour_ref[1])
    rate += where((t_gap == 1) & (s_gap == 0), diff_ref[2] - cour_ref[2])
    rate += where((t_gap == third_len - 1) & (s_gap == 0), diff_ref[2] + cour_ref[2])
    for which, part in enumerate((1.0 / 3.0, 0.5, 1.0)):
        rate_high[which], rate_low[which] = halves(rate * part)

    kept = divides(s_col, cut_ref[0, 1]) * divides(t_col, cut_ref[0, 2])
    entry = surplus_entry(s_row, s_col, second_len) * surplus_entry(t_row, t_col, third_len)
    surplus_ref[...] = (kept * weight_ref[0].astype(jnp.float32) * entry).astype(jnp.bfloat16)
    entry = restore_entry(s_col, s_row, second_len) * restore_entry(t_col, t_row, third_len)
    restore_ref[...] = (kept * entry).astype(jnp.bfloat16)


def tables(cutoffs, weights, diffusion, courant, second_len, third_len):
    lanes = second_len * third_len
    one = jax.ShapeDtypeStruct((lanes, lanes), jnp.bfloat16)
    three = jax.ShapeDtypeStruct((3, lanes, lanes), jnp.bfloat16)
    outs = [three, three, one, one]
    return pl.pallas_call(
        functools.partial(tables_kernel, (second_len, third_len)),
        out_shape=outs,
        in_specs=[SMEM] * 4,
        out_specs=[VMEM] * 4,
        compiler_params=params(*outs),
    )(cutoffs, weights, diffusion, courant)


def windows_kernel(dom, u_ref, *refs):
    out_refs, ext = refs[:-1], refs[-1]
    rows, _, length = u_ref.shape
    block = length // dom
    place = lax.axis_index("dom")
    for r in range(rows):
        turned_row = u_ref[r].T
        ext[r, pl.ds(HALO, length), :] = turned_row
        ext[r, pl.ds(0, HALO), :] = turned_row[length - HALO :]
        ext[r, pl.ds(HALO + length, HALO), :] = turned_row[:HALO]
    for k in range(dom):
        start = pl.multiple_of((place ^ k) * block, TILE)
        for c in range(CHAINS):
            out = out_refs[c * dom + k]
            out[...] = ext[:, pl.ds(start, out.shape[1]), :]
            start += out.shape[1]


def windows(u, dom):
    rows, lanes, length = u.shape
    sub = length // dom // CHAINS
    outs = [floats(rows, sub + 2 * HALO if c == 0 else sub, lanes) for c in range(CHAINS) for _ in range(dom)]
    ext = (rows, length + 2 * HALO, lanes)
    sent = pl.pallas_call(
        functools.partial(windows_kernel, dom),
        out_shape=outs,
        in_specs=[VMEM],
        out_specs=[VMEM] * len(outs),
        scratch_shapes=[pltpu.VMEM(ext, jnp.float32)],
        compiler_params=params(u, floats(*ext), *outs),
    )(u)
    return [sent[c * dom : (c + 1) * dom] for c in range(CHAINS)]


def evolve_kernel(plan, cut_ref, diff_ref, cour_ref, rate_high, rate_low, lane_surplus, *refs):
    dom, order, chunk, arrays = plan
    in_refs, refs = refs[: dom * arrays], refs[dom * arrays :]
    out_refs, (u, w1, w2) = refs[:-3], refs[-3:]
    rows = in_refs[0].shape[0]
    tiles, total, width, _ = u.shape
    width -= 3 * TILE
    sub = width - 2 * HALO
    place = lax.axis_index("dom")
    body_rows = pl.ds(TILE, width)
    for k in range(dom):
        at, need = TILE + width, width
        for a in reversed(range(arrays)):
            part = in_refs[a * dom + k]
            take = min(need, part.shape[1])
            at, need = at - take, need - take
            for h in range(tiles):
                u[h, pl.ds((place ^ k) * rows, rows), pl.ds(at, take), :] = part[
                    :, pl.ds(part.shape[1] - take, take), pl.ds(h * LANES, LANES)
                ]
    spare = jnp.zeros((tiles, total, TILE, LANES), jnp.float32)
    for ref in (u, w1, w2):
        ref[:, :, pl.ds(0, TILE), :] = spare
        ref[:, :, pl.ds(TILE + width, TILE), :] = spare

    def flat_rows(source, start):
        return jnp.concatenate(
            [
                jnp.concatenate([source[h, start + r, body_rows, :] for h in range(tiles)], axis=1)
                for r in range(chunk)
            ],
            axis=0,
        )

    def cut_rows(product, r, h):
        return product[r * width : (r + 1) * width, h * LANES : (h + 1) * LANES]

    def loop(body):
        group = min(GROUP, total)

        def rows_of(start):
            for c in range(0, group, chunk):
                body(start + c)

        if group == total:
            rows_of(0)
        else:
            lax.fori_loop(0, total // group, lambda g, carry: (rows_of(g * group), carry)[1], 0)

    def around(i):
        return i % total if isinstance(i, int) else lax.rem(i, total)

    def stage(source, target, which, part):
        first = [part * (diff_ref[d] - cour_ref[d]) for d in (0, 3)]
        second = [part * (diff_ref[d] + cour_ref[d]) for d in (0, 3)]

        def body(start):
            product = split_product(flat_rows(source, start), rate_high[which], rate_low[which])
            for r in range(chunk):
                i = start + r
                above = around(i + 1) if r + 1 == chunk else i + 1
                below = around(i + total - 1) if r == 0 else i - 1
                for h in range(tiles):
                    target[h, i, body_rows, :] = (
                        u[h, i, body_rows, :]
                        + cut_rows(product, r, h)
                        + (first[0] * source[h, above, body_rows, :] + second[0] * source[h, below, body_rows, :])
                        + (
                            first[1] * source[h, i, pl.ds(TILE + 1, width), :]
                            + second[1] * source[h, i, pl.ds(TILE - 1, width), :]
                        )
                    )

        loop(body)

    for _ in range(STEPS):
        stage(u, w1, 0, 1.0 / 3.0)
        stage(w1, w2, 1, 0.5)
        stage(w2, u, 2, 1.0)

    cell = lax.broadcasted_iota(jnp.int32, (sub, LANES), 0)
    low = jnp.bitwise_and(cell, 3)
    kept = divides(cell, cut_ref[0, 3])
    near = jnp.where(jnp.bitwise_and(low, 1) == 1, -0.5, 0.0) * kept
    far = jnp.where(low == 2, -0.5, 0.0) * kept

    def lines(start):
        product = split_product(flat_rows(u, start), lane_surplus[...])
        for r in range(chunk):
            for h in range(tiles):
                w1[h, start + r, body_rows, :] = cut_rows(product, r, h)
                at = [w1[h, start + r, pl.ds(TILE + HALO + by, sub), :] for by in (-2, -1, 0, 1, 2)]
                w2[h, start + r, pl.ds(TILE, sub), :] = (
                    kept * at[2] + near * (at[1] + at[3]) + far * (at[0] + at[4])
                )

    loop(lines)

    pieces = len(order)
    depth = sub // pieces
    count = pieces.bit_length() - 1
    scales = {2: divides(jnp.int32(2), cut_ref[0, 0]), 1: divides(jnp.int32(1), cut_ref[0, 0])}
    for slot, q in enumerate(order):
        offset = pl.multiple_of(TILE + piece_at(q, count) * depth, TILE)
        out, index = out_refs[slot // out_refs[0].shape[0]], slot % out_refs[0].shape[0]
        for h in range(tiles):
            line = [w2[h, i, pl.ds(offset, depth), :] for i in range(total)]
            for i in range(total):
                value = line[i]
                if i % 4:
                    hop = 2 if i % 2 == 0 else 1
                    value = scales[hop] * (value - 0.5 * (line[i - hop] + line[(i + hop) % total]))
                out[index, i, :, pl.ds(h * LANES, LANES)] = value


def evolve(cutoffs, diffusion, courant, mats, parts, order):
    dom, arrays = len(parts[0]), len(parts)
    rows, lanes = parts[0][0].shape[0], parts[0][0].shape[2]
    sub = min(p[0].shape[1] for p in parts)
    if arrays == 1:
        sub -= 2 * HALO
    total = rows * dom
    width = sub + 2 * HALO
    pieces = len(order)
    kept = max(pieces // 2, 1)
    outs = [floats(kept, total, sub // pieces, lanes)] * min(pieces, 2)
    state = (lanes // LANES, total, width + 3 * TILE, LANES)
    chunk = min(4, total)
    flat = [p for part in parts for p in part]
    return pl.pallas_call(
        functools.partial(evolve_kernel, (dom, order, chunk, arrays)),
        out_shape=outs,
        in_specs=[SMEM] * 3 + [VMEM] * (3 + len(flat)),
        out_specs=[VMEM] * len(outs),
        scratch_shapes=[pltpu.VMEM(state, jnp.float32)] * 3,
        compiler_params=params(*flat, *outs, *[floats(*state)] * 3),
    )(cutoffs, diffusion, courant, *mats, *flat)


def rows_kernel(dom, scale, *refs):
    in_refs, out_refs = refs[:-2], refs[-2:]
    total = in_refs[0].shape[0]
    rows = total // dom
    place = lax.axis_index("dom")

    def row(i):
        value = in_refs[0][pl.ds(i, 1)]
        for ref in in_refs[1:]:
            value += ref[pl.ds(i, 1)]
        return value * scale

    for k in range(dom):
        first = (place ^ k) * rows
        out, slot = out_refs[k // (dom // 2)], k % (dom // 2)
        for r in range(rows + 1):
            i = first + r if r < rows else lax.rem(first + rows, total)
            out[slot, pl.ds(r, 1)] = row(i)


def rows_for(dom, scale, addends):
    total, depth, lanes = addends[0].shape
    outs = [floats(dom // 2, total // dom + 1, depth, lanes)] * 2
    return pl.pallas_call(
        functools.partial(rows_kernel, dom, scale),
        out_shape=outs,
        in_specs=[VMEM] * len(addends),
        out_specs=[VMEM] * 2,
        compiler_params=params(*addends, *outs),
    )(*addends)


def exchange_rows(keep, send, dom):
    sources = [0]
    keep, send = keep[:, None], send[:, None]
    bit = dom // 2
    while True:
        held = jnp.concatenate([keep, swapped(send, "dom", bit)], axis=1)
        sources = sources + [s | bit for s in sources]
        if bit == 1:
            return held[0], tuple(sources)
        bit = bit // 2
        keep, send = held[:bit], held[bit:]


def restore_kernel(plan, cut_ref, lane_restore, *refs):
    dom, groups = plan
    in_refs, out_ref, (summed, lined, held, written) = refs[:-5], refs[-5], refs[-4:]
    rows, lanes, length = out_ref.shape
    tiles = lanes // LANES
    place = lax.axis_index("dom")
    block = length // dom
    for ref, (chain, count, slots, sources) in zip(in_refs, groups):
        depth = block // CHAINS >> count
        for s, q in enumerate(slots):
            piece = chain * (block // CHAINS) + piece_at(q, count) * depth
            for m, k in enumerate(sources):
                at = pl.multiple_of(TILE + (place ^ k) * block + piece, TILE)
                for h in range(tiles):
                    summed[h, :, pl.ds(at, depth), :] = ref[s, m, :, :, pl.ds(h * LANES, LANES)]
    summed[:, :, pl.ds(TILE + length, TILE), :] = summed[:, :, pl.ds(TILE, TILE), :]
    summed[:, :, pl.ds(0, TILE), :] = jnp.zeros((tiles, rows + 1, TILE, LANES), jnp.float32)
    lined[:, :, pl.ds(0, TILE), :] = jnp.zeros((tiles, rows, TILE, LANES), jnp.float32)

    cell = lax.broadcasted_iota(jnp.int32, (length, LANES), 0)
    low = jnp.bitwise_and(cell, 3)
    kept = divides(cell, cut_ref[0, 3])
    far = jnp.where(low == 2, 0.5, 0.0)
    near = jnp.where(jnp.bitwise_and(low, 1) == 1, 0.5, 0.0)
    one = divides(jnp.int32(1), cut_ref[0, 0])
    two = divides(jnp.int32(2), cut_ref[0, 0])

    def along_rows(target, scale, before, after):
        for h in range(tiles):
            summed[h, target] = scale * summed[h, target] + 0.5 * (summed[h, before] + summed[h, after])

    def along_cells(r):
        for h in range(tiles):
            at = [summed[h, r, pl.ds(TILE + by, length), :] for by in (-2, 0, 2)]
            lined[h, r, pl.ds(TILE, length), :] = kept * at[1] + far * (at[0] + at[2])
            lined[h, r, pl.ds(TILE + length, TILE), :] = summed[h, r, pl.ds(TILE, TILE), :]
        line = []
        for h in range(tiles):
            at = [lined[h, r, pl.ds(TILE + by, length), :] for by in (-1, 0, 1)]
            line.append(at[1] + near * (at[0] + at[2]))
        high, low_part = halves(jnp.concatenate(line, axis=1))
        dims = (((1,), (1,)), ((), ()))
        dot = functools.partial(lax.dot_general, dimension_numbers=dims, preferred_element_type=jnp.float32)
        held[r] = dot(lane_restore[...], high) + dot(lane_restore[...], low_part)

    writes = [pltpu.make_async_copy(held.at[r], out_ref.at[r], written.at[r]) for r in range(rows)]
    for r in range(0, rows, 4):
        along_rows(r + 2, two, r, r + 4)
        along_rows(r + 1, one, r, r + 2)
        along_rows(r + 3, one, r + 2, r + 4)
        for i in range(r, r + 4):
            along_cells(i)
            writes[i].start()
    for write in writes:
        write.wait()


def restore(cutoffs, lane_restore, arrays, groups, dom, rows, lanes, length):
    out = floats(rows, lanes, length)
    summed, lined = [(lanes // LANES, n, length + 2 * TILE, LANES) for n in (rows + 1, rows)]
    return pl.pallas_call(
        functools.partial(restore_kernel, (dom, groups)),
        out_shape=out,
        in_specs=[SMEM, VMEM] + [VMEM] * len(arrays),
        out_specs=FAR,
        scratch_shapes=[
            pltpu.VMEM(summed, jnp.float32),
            pltpu.VMEM(lined, jnp.float32),
            pltpu.VMEM(out.shape, jnp.float32),
            pltpu.SemaphoreType.DMA((rows,)),
        ],
        compiler_params=params(*arrays, out, floats(*summed), floats(*lined)),
    )(cutoffs, lane_restore, *arrays)


def slot_order(count):
    order = [0]
    for i in reversed(range(count)):
        order = order + [q | 1 << i for q in order]
    return tuple(order)


def grid_sum(first, count, bits):
    state = list(first)
    for i in range(count - 1):
        added = state[0] + swapped_in_turn(state[1], i, count)
        half = added.shape[0] // 2
        state = [added[:half], added[half:]]
    addends = [state[0][0]]
    if count:
        addends.append(swapped_in_turn(state[1], count - 1, count)[0])
    for i, bit in enumerate(bits[count:], count):
        own = sum(addends[1:], addends[0])
        addends = [own, swapped(own, "grid", bit)]
    return addends


def shards(fields, cutoffs, weights, diffusion, courant):
    rows, second_len, third_len, length = fields.shape[1:]
    lanes = second_len * third_len
    dom, grids = lax.axis_size("dom"), lax.axis_size("grid")
    sub = length // dom // CHAINS
    bits = [1 << i for i in range(grids.bit_length() - 1)]
    count = max(min(len(bits) - 1, (sub // TILE).bit_length() - 1), 0)
    order = slot_order(count)

    sent = windows(fields.reshape(rows, lanes, length), dom)
    mats = tables(cutoffs, weights, diffusion, courant, second_len, third_len)
    parts = []
    for chain, s in zip("ab", sent):
        moved = [swapped(s[k], "dom", k) for k in reversed(range(1, dom))]
        parts.append([s[0]] + moved[::-1])

    arrays, groups = [], []
    for c in range(CHAINS):
        chain = "ab"[c]
        first = evolve(cutoffs, diffusion, courant, mats[:3], parts[: c + 1][-2:], order)
        addends = grid_sum(first, count, bits)
        needed = rows_for(dom, 1.0 / grids, addends)
        home, sources = exchange_rows(*needed, dom)
        held = [((0,), home[None])]
        for i in reversed(range(count)):
            for slots, piece in list(held):
                arrived = swapped_in_turn(piece, i, count)
                held.append((tuple(q | 1 << i for q in slots), arrived))
            if i and chain not in EAGER:
                slots = sum((slots for slots, _ in held), ())
                held = [(slots, jnp.concatenate([piece for _, piece in held]))]
        for slots, piece in held:
            arrays.append(piece)
            groups.append((c, count, slots, sources))
    out = restore(cutoffs, mats[3], arrays, tuple(groups), dom, rows, lanes, length)
    return out.reshape(1, rows, second_len, third_len, length)


def solution(mesh):
    in_specs = (P("grid", "dom", None, None, None), P("grid", None), P("grid"), P(), P())
    out_specs = P("grid", "dom", None, None, None)

    return jax.shard_map(shards, mesh=mesh, in_specs=in_specs, out_specs=out_specs, check_vma=False)
```

profile of v0, /device:TPU:0, one launch (start us, length us, event | category | flops | bytes accessed | tf_op | source)
XLA Modules:
  0.0 72.7 jit_solution(11854165617873533881)
XLA Ops:
  0.0 1.2 %copy-done = f32[1,4,16,16,256]{4,3,2,1,0:T(8,128)S(1)} copy-done((f32[1,4,16,16,256]{4,3,2,1,0:T(8,128)S(1)}, f32[1,4,16,16,256]{4,3,2,1,0:T(8,128)}, u32[]{:S(2)}) %copy-start) | copy-done | bytes 1048600
  1.2 0.5 shard_map.56
  1.7 0.6 collective-permute-start.11
  2.3 0.1 collective-permute-start
  2.3 2.9 %collective-permute-start.1 = (f32[4,48,256]{2,1,0:T(8,128)S(1)}, f32[4,48,256]{2,1,0:T(8,128)S(1)}, u32[]{:S(2)}, u32[]{:S(2)}) collective-permute-start(f32[4,48,256]{2,1,0:T(8,128)S(1)} %get-tuple-element.31), channel_id=1, source_target_pairs={{0,2},{1,3},{2,0},{3,1},{4,6},{5,7},{6,4},{7,5},{8,10},{9,11},{10,... | collective-permute-start | bytes 589832 | tf_op jit(solution)/shard_map/ppermute | solution.py:35
  5.2 0.0 collective-permute-start.2
  5.2 1.4 %collective-permute-start.12 = (f32[4,32,256]{2,1,0:T(8,128)S(1)}, f32[4,32,256]{2,1,0:T(8,128)S(1)}, u32[]{:S(2)}, u32[]{:S(2)}) collective-permute-start(f32[4,32,256]{2,1,0:T(8,128)S(1)} %get-tuple-element.39), channel_id=1, source_target_pairs={{0,2},{1,3},{2,0},{3,1},{4,6},{5,7},{6,4},{7,5},{8,10},{9,11},{10,... | collective-permute-start | bytes 393224 | tf_op jit(solution)/shard_map/ppermute | solution.py:35
  6.7 0.0 collective-permute-done.11.refs_5_
  6.7 0.4 collective-permute-start.13
  7.8 1.7 %shard_map.55 = (bf16[3,256,256]{2,1,0:T(8,128)(2,1)S(1)}, bf16[3,256,256]{2,1,0:T(8,128)(2,1)S(1)}, bf16[256,256]{1,0:T(8,128)(2,1)S(1)}, bf16[256,256]{1,0:T(8,128)(2,1)S(1)}) custom-call(s32[1,4]{1,0:T(1,128)S(1)} %copy-done.1, s32[1]{0:T(128)S(6)} %copy.6.weight_ref, f32[4]{0:T(128)S(1)} %copy-done.2, f32[4]{0:T(128)S(1)} %copy-done.3), custom_call_target="tpu_custom_call" | custom-call | tf_op jit(solution)/shard_map/pallas_call | solution.py:132
  9.5 8.5 %collective-permute-done.12.refs_6_ = f32[4,32,256]{2,1,0:T(8,128)S(1)} collective-permute-done((f32[4,32,256]{2,1,0:T(8,128)S(1)}, f32[4,32,256]{2,1,0:T(8,128)S(1)}, u32[]{:S(2)}, u32[]{:S(2)}) %collective-permute-start.12) | collective-permute-done | bytes 131104 | tf_op jit(solution)/shard_map/ppermute | solution.py:35
  18.0 1.6 %collective-permute-done.13.refs_7_ = f32[4,32,256]{2,1,0:T(8,128)S(1)} collective-permute-done((f32[4,32,256]{2,1,0:T(8,128)S(1)}, f32[4,32,256]{2,1,0:T(8,128)S(1)}, u32[]{:S(2)}, u32[]{:S(2)}) %collective-permute-start.13) | collective-permute-done | bytes 131104 | tf_op jit(solution)/shard_map/ppermute | solution.py:35
  19.6 0.0 collective-permute-done.refs_1_
  19.6 0.0 collective-permute-done.1.refs_2_
  19.6 0.0 collective-permute-done.2.refs_3_
  19.6 3.7 %shard_map.59 = (f32[2,16,8,256]{3,2,1,0:T(8,128)S(1)}, f32[2,16,8,256]{3,2,1,0:T(8,128)S(1)}) custom-call(s32[1,4]{1,0:T(1,128)S(1)} %copy-done.1, f32[4]{0:T(128)S(1)} %copy-done.2, f32[4]{0:T(128)S(1)} %copy-done.3, bf16[3,256,256]{2,1,0:T(8,128)(2,1)S(1)} %get-tuple-element.26.rate_high, bf16[3,256,256]{2,1,0:T(8,128)(2,1)S(1)} %get-tuple-element.27.rate_low, ...), custom_call_target="tpu_custom_call" | custom-call | tf_op jit(solution)/shard_map/pallas_call | solution.py:304
  23.3 1.6 %collective-permute-start.14 = (f32[2,16,8,256]{3,2,1,0:T(8,128)S(1)}, f32[2,16,8,256]{3,2,1,0:T(8,128)S(1)}, u32[]{:S(2)}, u32[]{:S(2)}) collective-permute-start(f32[2,16,8,256]{3,2,1,0:T(8,128)S(1)} %get-tuple-element.42), channel_id=1, source_target_pairs={{0,4},{1,9},{2,6},{3,11},{4,0},{5,13},{6,2},{7,15},{8,12},{9,1},{1... | collective-permute-start | bytes 786440 | tf_op jit(solution)/shard_map/ppermute | solution.py:48
  24.9 3.7 %shard_map.57 = (f32[2,16,8,256]{3,2,1,0:T(8,128)S(1)}, f32[2,16,8,256]{3,2,1,0:T(8,128)S(1)}) custom-call(s32[1,4]{1,0:T(1,128)S(1)} %copy-done.1, f32[4]{0:T(128)S(1)} %copy-done.2, f32[4]{0:T(128)S(1)} %copy-done.3, bf16[3,256,256]{2,1,0:T(8,128)(2,1)S(1)} %get-tuple-element.26.rate_high, bf16[3,256,256]{2,1,0:T(8,128)(2,1)S(1)} %get-tuple-element.27.rate_low, ...), custom_call_target="tpu_custom_call" | custom-call | tf_op jit(solution)/shard_map/pallas_call | solution.py:304
  28.6 0.6 collective-permute-start.3
  29.2 0.6 collective-permute-done.14
  29.8 1.6 %collective-permute-start.15 = (f32[1,16,8,256]{3,2,1,0:T(8,128)S(1)}, f32[1,16,8,256]{3,2,1,0:T(8,128)S(1)}, u32[]{:S(2)}, u32[]{:S(2)}) collective-permute-start(f32[1,16,8,256]{3,2,1,0:T(8,128)S(1)} %slice.37), channel_id=1, source_target_pairs={{0,8},{1,5},{2,10},{3,7},{4,12},{5,1},{6,14},{7,3},{8,0},{9,13},{1... | collective-permute-start | bytes 393224 | tf_op jit(solution)/shard_map/ppermute | solution.py:48
  31.4 4.9 %collective-permute-done.3 = f32[2,16,8,256]{3,2,1,0:T(8,128)S(1)} collective-permute-done((f32[2,16,8,256]{3,2,1,0:T(8,128)S(1)}, f32[2,16,8,256]{3,2,1,0:T(8,128)S(1)}, u32[]{:S(2)}, u32[]{:S(2)}) %collective-permute-start.3) | collective-permute-done | bytes 262176 | tf_op jit(solution)/shard_map/ppermute | solution.py:48
  36.4 1.7 %collective-permute-start.4 = (f32[1,16,8,256]{3,2,1,0:T(8,128)S(1)}, f32[1,16,8,256]{3,2,1,0:T(8,128)S(1)}, u32[]{:S(2)}, u32[]{:S(2)}) collective-permute-start(f32[1,16,8,256]{3,2,1,0:T(8,128)S(1)} %slice.33), channel_id=1, source_target_pairs={{0,8},{1,5},{2,10},{3,7},{4,12},{5,1},{6,14},{7,3},{8,0},{9,13},{1... | collective-permute-start | bytes 393224 | tf_op jit(solution)/shard_map/ppermute | solution.py:48
  38.2 2.6 %collective-permute-start.16 = (f32[16,8,256]{2,1,0:T(8,128)S(1)}, f32[16,8,256]{2,1,0:T(8,128)S(1)}, u32[]{:S(2)}, u32[]{:S(2)}) collective-permute-start(f32[16,8,256]{2,1,0:T(8,128)S(1)} %fusion.refs_0_), channel_id=1, source_target_pairs={{0,16},{4,20},{8,24},{12,28},{16,0},{20,4},{24,8},{28,12},{1,17},{... | collective-permute-start | bytes 393224 | tf_op jit(solution)/shard_map/ppermute | solution.py:35
  40.8 1.8 %collective-permute-done.4 = f32[1,16,8,256]{3,2,1,0:T(8,128)S(1)} collective-permute-done((f32[1,16,8,256]{3,2,1,0:T(8,128)S(1)}, f32[1,16,8,256]{3,2,1,0:T(8,128)S(1)}, u32[]{:S(2)}, u32[]{:S(2)}) %collective-permute-start.4) | collective-permute-done | bytes 131104 | tf_op jit(solution)/shard_map/ppermute | solution.py:48
  42.7 2.8 %collective-permute-start.5 = (f32[16,8,256]{2,1,0:T(8,128)S(1)}, f32[16,8,256]{2,1,0:T(8,128)S(1)}, u32[]{:S(2)}, u32[]{:S(2)}) collective-permute-start(f32[16,8,256]{2,1,0:T(8,128)S(1)} %fusion.1.refs_0_), channel_id=1, source_target_pairs={{0,16},{4,20},{8,24},{12,28},{16,0},{20,4},{24,8},{28,12},{1,17},{... | collective-permute-start | bytes 393224 | tf_op jit(solution)/shard_map/ppermute | solution.py:35
  45.5 4.0 %collective-permute-done.16.refs_1_ = f32[16,8,256]{2,1,0:T(8,128)S(1)} collective-permute-done((f32[16,8,256]{2,1,0:T(8,128)S(1)}, f32[16,8,256]{2,1,0:T(8,128)S(1)}, u32[]{:S(2)}, u32[]{:S(2)}) %collective-permute-start.16) | collective-permute-done | bytes 131104 | tf_op jit(solution)/shard_map/ppermute | solution.py:35
  49.5 1.6 %collective-permute-start.17 = (f32[2,1,5,8,256]{4,3,2,1,0:T(8,128)S(1)}, f32[2,1,5,8,256]{4,3,2,1,0:T(8,128)S(1)}, u32[]{:S(2)}, u32[]{:S(2)}) collective-permute-start(f32[2,1,5,8,256]{4,3,2,1,0:T(8,128)S(1)} %bitcast.14), channel_id=1, source_target_pairs={{0,2},{1,3},{2,0},{3,1},{4,6},{5,7},{6,4},{7,5},{8,10},{9,11},{10,... | collective-permute-start | bytes 245768 | tf_op jit(solution)/shard_map/ppermute | solution.py:35
  51.1 0.0 collective-permute-done.5.refs_1_
  51.1 1.6 %collective-permute-start.6 = (f32[2,1,5,8,256]{4,3,2,1,0:T(8,128)S(1)}, f32[2,1,5,8,256]{4,3,2,1,0:T(8,128)S(1)}, u32[]{:S(2)}, u32[]{:S(2)}) collective-permute-start(f32[2,1,5,8,256]{4,3,2,1,0:T(8,128)S(1)} %bitcast.13), channel_id=1, source_target_pairs={{0,2},{1,3},{2,0},{3,1},{4,6},{5,7},{6,4},{7,5},{8,10},{9,11},{10,... | collective-permute-start | bytes 245768 | tf_op jit(solution)/shard_map/ppermute | solution.py:35
  52.7 1.7 %collective-permute-done.17 = f32[2,1,5,8,256]{4,3,2,1,0:T(8,128)S(1)} collective-permute-done((f32[2,1,5,8,256]{4,3,2,1,0:T(8,128)S(1)}, f32[2,1,5,8,256]{4,3,2,1,0:T(8,128)S(1)}, u32[]{:S(2)}, u32[]{:S(2)}) %collective-permute-start.17) | collective-permute-done | bytes 81952 | tf_op jit(solution)/shard_map/ppermute | solution.py:35
  54.4 0.1 collective-permute-start.18
  54.5 1.1 %collective-permute-done.6 = f32[2,1,5,8,256]{4,3,2,1,0:T(8,128)S(1)} collective-permute-done((f32[2,1,5,8,256]{4,3,2,1,0:T(8,128)S(1)}, f32[2,1,5,8,256]{4,3,2,1,0:T(8,128)S(1)}, u32[]{:S(2)}, u32[]{:S(2)}) %collective-permute-start.6) | collective-permute-done | bytes 81952 | tf_op jit(solution)/shard_map/ppermute | solution.py:35
  55.6 0.1 collective-permute-start.7
  55.7 0.1 collective-permute-done.18
  55.8 0.7 collective-permute-start.19
  56.5 0.5 collective-permute-done.7
  57.0 1.0 %collective-permute-start.8 = (f32[1,4,5,8,256]{4,3,2,1,0:T(8,128)S(1)}, f32[1,4,5,8,256]{4,3,2,1,0:T(8,128)S(1)}, u32[]{:S(2)}, u32[]{:S(2)}) collective-permute-start(f32[1,4,5,8,256]{4,3,2,1,0:T(8,128)S(1)} %pad_maximum_fusion.refs_0_), channel_id=1, source_target_pairs={{0,8},{1,5},{2,10},{3,7},{4,12},{5,1},{6,14},{7,3},{8,0},{9,13},{1... | collective-permute-start | bytes 491528 | tf_op jit(solution)/shard_map/ppermute | solution.py:48
  58.0 1.3 %collective-permute-start.20 = (f32[1,4,5,8,256]{4,3,2,1,0:T(8,128)S(1)}, f32[1,4,5,8,256]{4,3,2,1,0:T(8,128)S(1)}, u32[]{:S(2)}, u32[]{:S(2)}) collective-permute-start(f32[1,4,5,8,256]{4,3,2,1,0:T(8,128)S(1)} %pad_maximum_fusion.1.refs_4_), channel_id=1, source_target_pairs={{0,4},{1,9},{2,6},{3,11},{4,0},{5,13},{6,2},{7,15},{8,12},{9,1},{1... | collective-permute-start | bytes 491528 | tf_op jit(solution)/shard_map/ppermute | solution.py:48
  59.3 0.7 %collective-permute-start.9 = (f32[1,4,5,8,256]{4,3,2,1,0:T(8,128)S(1)}, f32[1,4,5,8,256]{4,3,2,1,0:T(8,128)S(1)}, u32[]{:S(2)}, u32[]{:S(2)}) collective-permute-start(f32[1,4,5,8,256]{4,3,2,1,0:T(8,128)S(1)} %pad_maximum_fusion.refs_0_), channel_id=1, source_target_pairs={{0,4},{1,9},{2,6},{3,11},{4,0},{5,13},{6,2},{7,15},{8,12},{9,1},{1... | collective-permute-start | bytes 491528 | tf_op jit(solution)/shard_map/ppermute | solution.py:48
  60.0 1.5 %collective-permute-done.19.refs_5_ = f32[1,4,5,8,256]{4,3,2,1,0:T(8,128)S(1)} collective-permute-done((f32[1,4,5,8,256]{4,3,2,1,0:T(8,128)S(1)}, f32[1,4,5,8,256]{4,3,2,1,0:T(8,128)S(1)}, u32[]{:S(2)}, u32[]{:S(2)}) %collective-permute-start.19) | collective-permute-done | bytes 163872 | tf_op jit(solution)/shard_map/ppermute | solution.py:48
  61.5 1.7 %collective-permute-start.21 = (f32[1,4,5,8,256]{4,3,2,1,0:T(8,128)S(1)}, f32[1,4,5,8,256]{4,3,2,1,0:T(8,128)S(1)}, u32[]{:S(2)}, u32[]{:S(2)}) collective-permute-start(f32[1,4,5,8,256]{4,3,2,1,0:T(8,128)S(1)} %collective-permute-done.19.refs_5_), channel_id=1, source_target_pairs={{0,4},{1,9},{2,6},{3,11},{4,0},{5,13},{6,2},{7,15},{8,12},{9,1},{1... | collective-permute-start | bytes 491528 | tf_op jit(solution)/shard_map/ppermute | solution.py:48
  63.1 1.8 %collective-permute-done.8.refs_1_ = f32[1,4,5,8,256]{4,3,2,1,0:T(8,128)S(1)} collective-permute-done((f32[1,4,5,8,256]{4,3,2,1,0:T(8,128)S(1)}, f32[1,4,5,8,256]{4,3,2,1,0:T(8,128)S(1)}, u32[]{:S(2)}, u32[]{:S(2)}) %collective-permute-start.8) | collective-permute-done | bytes 163872 | tf_op jit(solution)/shard_map/ppermute | solution.py:48
  65.0 1.7 %collective-permute-start.10 = (f32[1,4,5,8,256]{4,3,2,1,0:T(8,128)S(1)}, f32[1,4,5,8,256]{4,3,2,1,0:T(8,128)S(1)}, u32[]{:S(2)}, u32[]{:S(2)}) collective-permute-start(f32[1,4,5,8,256]{4,3,2,1,0:T(8,128)S(1)} %collective-permute-done.8.refs_1_), channel_id=1, source_target_pairs={{0,4},{1,9},{2,6},{3,11},{4,0},{5,13},{6,2},{7,15},{8,12},{9,1},{1... | collective-permute-start | bytes 491528 | tf_op jit(solution)/shard_map/ppermute | solution.py:48
  66.7 0.0 collective-permute-done.20.refs_6_
  66.7 1.0 %collective-permute-done.21.refs_7_ = f32[1,4,5,8,256]{4,3,2,1,0:T(8,128)S(1)} collective-permute-done((f32[1,4,5,8,256]{4,3,2,1,0:T(8,128)S(1)}, f32[1,4,5,8,256]{4,3,2,1,0:T(8,128)S(1)}, u32[]{:S(2)}, u32[]{:S(2)}) %collective-permute-start.21) | collective-permute-done | bytes 163872 | tf_op jit(solution)/shard_map/ppermute | solution.py:48
  67.7 2.7 %collective-permute-done.10.refs_3_ = f32[1,4,5,8,256]{4,3,2,1,0:T(8,128)S(1)} collective-permute-done((f32[1,4,5,8,256]{4,3,2,1,0:T(8,128)S(1)}, f32[1,4,5,8,256]{4,3,2,1,0:T(8,128)S(1)}, u32[]{:S(2)}, u32[]{:S(2)}) %collective-permute-start.10) | collective-permute-done | bytes 163872 | tf_op jit(solution)/shard_map/ppermute | solution.py:48
  70.3 2.4 %shard_map.61 = f32[4,256,256]{2,1,0:T(8,128)} custom-call(s32[1,4]{1,0:T(1,128)S(1)} %copy-done.1, bf16[256,256]{1,0:T(8,128)(2,1)S(1)} %get-tuple-element.25.lane_restore, f32[1,4,5,8,256]{4,3,2,1,0:T(8,128)S(1)} %pad_maximum_fusion.refs_0_, f32[1,4,5,8,256]{4,3,2,1,0:T(8,128)S(1)} %collective-permute-done.8.refs_1_, ...), custom_call_target="tpu_custom_call" | custom-call | tf_op jit(solution)/shard_map/pallas_call | solution.py:419
  (21 shorter events, 0.2 us)
Async XLA Ops:
  0.0 1.2 %copy-start = (f32[1,4,16,16,256]{4,3,2,1,0:T(8,128)S(1)}, f32[1,4,16,16,256]{4,3,2,1,0:T(8,128)}, u32[]{:S(2)}) copy-start(f32[1,4,16,16,256]{4,3,2,1,0:T(8,128)} %param.5) | copy-start | bytes 3145732
  1.7 5.0 %collective-permute-start.11 = (f32[4,32,256]{2,1,0:T(8,128)S(1)}, f32[4,32,256]{2,1,0:T(8,128)S(1)}, u32[]{:S(2)}, u32[]{:S(2)}) collective-permute-start(f32[4,32,256]{2,1,0:T(8,128)S(1)} %get-tuple-element.38), channel_id=1, source_target_pairs={{0,1},{1,0},{2,3},{3,2},{4,5},{5,4},{6,7},{7,6},{8,9},{9,8},{10,11... | collective-permute-start | bytes 393224 | tf_op jit(solution)/shard_map/ppermute | solution.py:35
  2.3 17.3 %collective-permute-start = (f32[4,48,256]{2,1,0:T(8,128)S(1)}, f32[4,48,256]{2,1,0:T(8,128)S(1)}, u32[]{:S(2)}, u32[]{:S(2)}) collective-permute-start(f32[4,48,256]{2,1,0:T(8,128)S(1)} %get-tuple-element.30), channel_id=1, source_target_pairs={{0,1},{1,0},{2,3},{3,2},{4,5},{5,4},{6,7},{7,6},{8,9},{9,8},{10,11... | collective-permute-start | bytes 589832 | tf_op jit(solution)/shard_map/ppermute | solution.py:35
  2.3 17.3 %collective-permute-start.1 = (f32[4,48,256]{2,1,0:T(8,128)S(1)}, f32[4,48,256]{2,1,0:T(8,128)S(1)}, u32[]{:S(2)}, u32[]{:S(2)}) collective-permute-start(f32[4,48,256]{2,1,0:T(8,128)S(1)} %get-tuple-element.31), channel_id=1, source_target_pairs={{0,2},{1,3},{2,0},{3,1},{4,6},{5,7},{6,4},{7,5},{8,10},{9,11},{10,... | collective-permute-start | bytes 589832 | tf_op jit(solution)/shard_map/ppermute | solution.py:35
  5.2 14.4 %collective-permute-start.2 = (f32[4,48,256]{2,1,0:T(8,128)S(1)}, f32[4,48,256]{2,1,0:T(8,128)S(1)}, u32[]{:S(2)}, u32[]{:S(2)}) collective-permute-start(f32[4,48,256]{2,1,0:T(8,128)S(1)} %get-tuple-element.32), channel_id=1, source_target_pairs={{0,3},{1,2},{2,1},{3,0},{4,7},{5,6},{6,5},{7,4},{8,11},{9,10},{10,... | collective-permute-start | bytes 589832 | tf_op jit(solution)/shard_map/ppermute | solution.py:35
  5.2 12.8 %collective-permute-start.12 = (f32[4,32,256]{2,1,0:T(8,128)S(1)}, f32[4,32,256]{2,1,0:T(8,128)S(1)}, u32[]{:S(2)}, u32[]{:S(2)}) collective-permute-start(f32[4,32,256]{2,1,0:T(8,128)S(1)} %get-tuple-element.39), channel_id=1, source_target_pairs={{0,2},{1,3},{2,0},{3,1},{4,6},{5,7},{6,4},{7,5},{8,10},{9,11},{10,... | collective-permute-start | bytes 393224 | tf_op jit(solution)/shard_map/ppermute | solution.py:35
  6.7 1.1 %copy-start.1 = (s32[1,4]{1,0:T(1,128)S(1)}, s32[1,4]{1,0:T(1,128)}, u32[]{:S(2)}) copy-start(s32[1,4]{1,0:T(1,128)} %cut_ref.7) | copy-start | bytes 52
  6.7 1.1 %copy-start.2 = (f32[4]{0:T(128)S(1)}, f32[4]{0:T(128)}, u32[]{:S(2)}) copy-start(f32[4]{0:T(128)} %diff_ref.5) | copy-start | bytes 52
  6.7 1.1 %copy-start.3 = (f32[4]{0:T(128)S(1)}, f32[4]{0:T(128)}, u32[]{:S(2)}) copy-start(f32[4]{0:T(128)} %cour_ref.5) | copy-start | bytes 52
  6.7 12.9 %collective-permute-start.13 = (f32[4,32,256]{2,1,0:T(8,128)S(1)}, f32[4,32,256]{2,1,0:T(8,128)S(1)}, u32[]{:S(2)}, u32[]{:S(2)}) collective-permute-start(f32[4,32,256]{2,1,0:T(8,128)S(1)} %get-tuple-element.40), channel_id=1, source_target_pairs={{0,3},{1,2},{2,1},{3,0},{4,7},{5,6},{6,5},{7,4},{8,11},{9,10},{10,... | collective-permute-start | bytes 393224 | tf_op jit(solution)/shard_map/ppermute | solution.py:35
  23.3 6.4 %collective-permute-start.14 = (f32[2,16,8,256]{3,2,1,0:T(8,128)S(1)}, f32[2,16,8,256]{3,2,1,0:T(8,128)S(1)}, u32[]{:S(2)}, u32[]{:S(2)}) collective-permute-start(f32[2,16,8,256]{3,2,1,0:T(8,128)S(1)} %get-tuple-element.42), channel_id=1, source_target_pairs={{0,4},{1,9},{2,6},{3,11},{4,0},{5,13},{6,2},{7,15},{8,12},{9,1},{1... | collective-permute-start | bytes 786440 | tf_op jit(solution)/shard_map/ppermute | solution.py:48
  28.6 7.8 %collective-permute-start.3 = (f32[2,16,8,256]{3,2,1,0:T(8,128)S(1)}, f32[2,16,8,256]{3,2,1,0:T(8,128)S(1)}, u32[]{:S(2)}, u32[]{:S(2)}) collective-permute-start(f32[2,16,8,256]{3,2,1,0:T(8,128)S(1)} %get-tuple-element.34), channel_id=1, source_target_pairs={{0,4},{1,9},{2,6},{3,11},{4,0},{5,13},{6,2},{7,15},{8,12},{9,1},{1... | collective-permute-start | bytes 786440 | tf_op jit(solution)/shard_map/ppermute | solution.py:48
  29.8 8.3 %collective-permute-start.15 = (f32[1,16,8,256]{3,2,1,0:T(8,128)S(1)}, f32[1,16,8,256]{3,2,1,0:T(8,128)S(1)}, u32[]{:S(2)}, u32[]{:S(2)}) collective-permute-start(f32[1,16,8,256]{3,2,1,0:T(8,128)S(1)} %slice.37), channel_id=1, source_target_pairs={{0,8},{1,5},{2,10},{3,7},{4,12},{5,1},{6,14},{7,3},{8,0},{9,13},{1... | collective-permute-start | bytes 393224 | tf_op jit(solution)/shard_map/ppermute | solution.py:48
  36.4 6.2 %collective-permute-start.4 = (f32[1,16,8,256]{3,2,1,0:T(8,128)S(1)}, f32[1,16,8,256]{3,2,1,0:T(8,128)S(1)}, u32[]{:S(2)}, u32[]{:S(2)}) collective-permute-start(f32[1,16,8,256]{3,2,1,0:T(8,128)S(1)} %slice.33), channel_id=1, source_target_pairs={{0,8},{1,5},{2,10},{3,7},{4,12},{5,1},{6,14},{7,3},{8,0},{9,13},{1... | collective-permute-start | bytes 393224 | tf_op jit(solution)/shard_map/ppermute | solution.py:48
  38.2 11.3 %collective-permute-start.16 = (f32[16,8,256]{2,1,0:T(8,128)S(1)}, f32[16,8,256]{2,1,0:T(8,128)S(1)}, u32[]{:S(2)}, u32[]{:S(2)}) collective-permute-start(f32[16,8,256]{2,1,0:T(8,128)S(1)} %fusion.refs_0_), channel_id=1, source_target_pairs={{0,16},{4,20},{8,24},{12,28},{16,0},{20,4},{24,8},{28,12},{1,17},{... | collective-permute-start | bytes 393224 | tf_op jit(solution)/shard_map/ppermute | solution.py:35
  42.7 8.4 %collective-permute-start.5 = (f32[16,8,256]{2,1,0:T(8,128)S(1)}, f32[16,8,256]{2,1,0:T(8,128)S(1)}, u32[]{:S(2)}, u32[]{:S(2)}) collective-permute-start(f32[16,8,256]{2,1,0:T(8,128)S(1)} %fusion.1.refs_0_), channel_id=1, source_target_pairs={{0,16},{4,20},{8,24},{12,28},{16,0},{20,4},{24,8},{28,12},{1,17},{... | collective-permute-start | bytes 393224 | tf_op jit(solution)/shard_map/ppermute | solution.py:35
  49.5 4.9 %collective-permute-start.17 = (f32[2,1,5,8,256]{4,3,2,1,0:T(8,128)S(1)}, f32[2,1,5,8,256]{4,3,2,1,0:T(8,128)S(1)}, u32[]{:S(2)}, u32[]{:S(2)}) collective-permute-start(f32[2,1,5,8,256]{4,3,2,1,0:T(8,128)S(1)} %bitcast.14), channel_id=1, source_target_pairs={{0,2},{1,3},{2,0},{3,1},{4,6},{5,7},{6,4},{7,5},{8,10},{9,11},{10,... | collective-permute-start | bytes 245768 | tf_op jit(solution)/shard_map/ppermute | solution.py:35
  51.1 4.5 %collective-permute-start.6 = (f32[2,1,5,8,256]{4,3,2,1,0:T(8,128)S(1)}, f32[2,1,5,8,256]{4,3,2,1,0:T(8,128)S(1)}, u32[]{:S(2)}, u32[]{:S(2)}) collective-permute-start(f32[2,1,5,8,256]{4,3,2,1,0:T(8,128)S(1)} %bitcast.13), channel_id=1, source_target_pairs={{0,2},{1,3},{2,0},{3,1},{4,6},{5,7},{6,4},{7,5},{8,10},{9,11},{10,... | collective-permute-start | bytes 245768 | tf_op jit(solution)/shard_map/ppermute | solution.py:35
  54.4 1.3 %collective-permute-start.18 = (f32[1,2,5,8,256]{4,3,2,1,0:T(8,128)S(1)}, f32[1,2,5,8,256]{4,3,2,1,0:T(8,128)S(1)}, u32[]{:S(2)}, u32[]{:S(2)}) collective-permute-start(f32[1,2,5,8,256]{4,3,2,1,0:T(8,128)S(1)} %get-tuple-element.46), channel_id=1, source_target_pairs={{0,1},{1,0},{2,3},{3,2},{4,5},{5,4},{6,7},{7,6},{8,9},{9,8},{10,11... | collective-permute-start | bytes 245768 | tf_op jit(solution)/shard_map/ppermute | solution.py:35
  55.6 1.3 %collective-permute-start.7 = (f32[1,2,5,8,256]{4,3,2,1,0:T(8,128)S(1)}, f32[1,2,5,8,256]{4,3,2,1,0:T(8,128)S(1)}, u32[]{:S(2)}, u32[]{:S(2)}) collective-permute-start(f32[1,2,5,8,256]{4,3,2,1,0:T(8,128)S(1)} %get-tuple-element.48), channel_id=1, source_target_pairs={{0,1},{1,0},{2,3},{3,2},{4,5},{5,4},{6,7},{7,6},{8,9},{9,8},{10,11... | collective-permute-start | bytes 245768 | tf_op jit(solution)/shard_map/ppermute | solution.py:35
  55.8 5.7 %collective-permute-start.19 = (f32[1,4,5,8,256]{4,3,2,1,0:T(8,128)S(1)}, f32[1,4,5,8,256]{4,3,2,1,0:T(8,128)S(1)}, u32[]{:S(2)}, u32[]{:S(2)}) collective-permute-start(f32[1,4,5,8,256]{4,3,2,1,0:T(8,128)S(1)} %pad_maximum_fusion.1.refs_4_), channel_id=1, source_target_pairs={{0,8},{1,5},{2,10},{3,7},{4,12},{5,1},{6,14},{7,3},{8,0},{9,13},{1... | collective-permute-start | bytes 491528 | tf_op jit(solution)/shard_map/ppermute | solution.py:48
  57.0 8.0 %collective-permute-start.8 = (f32[1,4,5,8,256]{4,3,2,1,0:T(8,128)S(1)}, f32[1,4,5,8,256]{4,3,2,1,0:T(8,128)S(1)}, u32[]{:S(2)}, u32[]{:S(2)}) collective-permute-start(f32[1,4,5,8,256]{4,3,2,1,0:T(8,128)S(1)} %pad_maximum_fusion.refs_0_), channel_id=1, source_target_pairs={{0,8},{1,5},{2,10},{3,7},{4,12},{5,1},{6,14},{7,3},{8,0},{9,13},{1... | collective-permute-start | bytes 491528 | tf_op jit(solution)/shard_map/ppermute | solution.py:48
  58.0 8.7 %collective-permute-start.20 = (f32[1,4,5,8,256]{4,3,2,1,0:T(8,128)S(1)}, f32[1,4,5,8,256]{4,3,2,1,0:T(8,128)S(1)}, u32[]{:S(2)}, u32[]{:S(2)}) collective-permute-start(f32[1,4,5,8,256]{4,3,2,1,0:T(8,128)S(1)} %pad_maximum_fusion.1.refs_4_), channel_id=1, source_target_pairs={{0,4},{1,9},{2,6},{3,11},{4,0},{5,13},{6,2},{7,15},{8,12},{9,1},{1... | collective-permute-start | bytes 491528 | tf_op jit(solution)/shard_map/ppermute | solution.py:48
  59.3 7.4 %collective-permute-start.9 = (f32[1,4,5,8,256]{4,3,2,1,0:T(8,128)S(1)}, f32[1,4,5,8,256]{4,3,2,1,0:T(8,128)S(1)}, u32[]{:S(2)}, u32[]{:S(2)}) collective-permute-start(f32[1,4,5,8,256]{4,3,2,1,0:T(8,128)S(1)} %pad_maximum_fusion.refs_0_), channel_id=1, source_target_pairs={{0,4},{1,9},{2,6},{3,11},{4,0},{5,13},{6,2},{7,15},{8,12},{9,1},{1... | collective-permute-start | bytes 491528 | tf_op jit(solution)/shard_map/ppermute | solution.py:48
  61.5 6.2 %collective-permute-start.21 = (f32[1,4,5,8,256]{4,3,2,1,0:T(8,128)S(1)}, f32[1,4,5,8,256]{4,3,2,1,0:T(8,128)S(1)}, u32[]{:S(2)}, u32[]{:S(2)}) collective-permute-start(f32[1,4,5,8,256]{4,3,2,1,0:T(8,128)S(1)} %collective-permute-done.19.refs_5_), channel_id=1, source_target_pairs={{0,4},{1,9},{2,6},{3,11},{4,0},{5,13},{6,2},{7,15},{8,12},{9,1},{1... | collective-permute-start | bytes 491528 | tf_op jit(solution)/shard_map/ppermute | solution.py:48
  65.0 5.3 %collective-permute-start.10 = (f32[1,4,5,8,256]{4,3,2,1,0:T(8,128)S(1)}, f32[1,4,5,8,256]{4,3,2,1,0:T(8,128)S(1)}, u32[]{:S(2)}, u32[]{:S(2)}) collective-permute-start(f32[1,4,5,8,256]{4,3,2,1,0:T(8,128)S(1)} %collective-permute-done.8.refs_1_), channel_id=1, source_target_pairs={{0,4},{1,9},{2,6},{3,11},{4,0},{5,13},{6,2},{7,15},{8,12},{9,1},{1... | collective-permute-start | bytes 491528 | tf_op jit(solution)/shard_map/ppermute | solution.py:48
where the time goes:
time: 72.9 us; the launch traced here: 72.7 us
  waiting for transfers between devices  31.9 us (44%)
  starting transfers between devices  26.6 us (36%)
  Pallas kernels  12 us (16%)
  local copies, waits for them, and re-layouts  1.26 us (2%)
  between operations  0.8 us (1%)
    ppermute x12, waiting for transfers between devices, swapped(): return lax.ppermute(x, axis, [(i, i ^ bit) for i in range(size)])  17.6 us
    ppermute x10, waiting for transfers between devices, swapped_in_turn(): return lax.ppermute(x, ('grid', 'dom'), pairs)  14.3 us
    ppermute x12, starting transfers between devices, swapped(): return lax.ppermute(x, axis, [(i, i ^ bit) for i in range(size)])  14.1 us
    ppermute x10, starting transfers between devices, swapped_in_turn(): return lax.ppermute(x, ('grid', 'dom'), pairs)  12.5 us
    pallas_call x2, Pallas kernels, evolve(): pl.pallas_call(functools.partial(evolve_kernel, (dom, order, chunk, array...  7.39 us
    pallas_call x1, Pallas kernels, restore(): pl.pallas_call(functools.partial(restore_kernel, (dom, groups)), out_shap...  2.42 us
    pallas_call x1, Pallas kernels, tables(): pl.pallas_call(functools.partial(tables_kernel, (second_len, third_len)),...  1.7 us
  transfers between devices with their start and end apart: 22, of which 14 were waited for; matrix products, arithmetic and copies ran while one was open for 0% of the time, Pallas kernels for 7%

commit v1 on v0

--- a/solution.py
+++ b/solution.py
@@ -312,7 +312,7 @@
 
 
 def rows_kernel(dom, scale, *refs):
-    in_refs, out_refs = refs[:-2], refs[-2:]
+    in_refs, out_refs = refs[:-dom], refs[-dom:]
     total = in_refs[0].shape[0]
     rows = total // dom
     place = lax.axis_index("dom")
@@ -325,35 +325,26 @@
 
     for k in range(dom):
         first = (place ^ k) * rows
-        out, slot = out_refs[k // (dom // 2)], k % (dom // 2)
         for r in range(rows + 1):
             i = first + r if r < rows else lax.rem(first + rows, total)
-            out[slot, pl.ds(r, 1)] = row(i)
+            out_refs[k][0, pl.ds(r, 1)] = row(i)
 
 
 def rows_for(dom, scale, addends):
     total, depth, lanes = addends[0].shape
-    outs = [floats(dom // 2, total // dom + 1, depth, lanes)] * 2
+    outs = [floats(1, total // dom + 1, depth, lanes)] * dom
     return pl.pallas_call(
         functools.partial(rows_kernel, dom, scale),
         out_shape=outs,
         in_specs=[VMEM] * len(addends),
-        out_specs=[VMEM] * 2,
+        out_specs=[VMEM] * dom,
         compiler_params=params(*addends, *outs),
     )(*addends)
 
 
-def exchange_rows(keep, send, dom):
-    sources = [0]
-    keep, send = keep[:, None], send[:, None]
-    bit = dom // 2
-    while True:
-        held = jnp.concatenate([keep, swapped(send, "dom", bit)], axis=1)
-        sources = sources + [s | bit for s in sources]
-        if bit == 1:
-            return held[0], tuple(sources)
-        bit = bit // 2
-        keep, send = held[:bit], held[bit:]
+def exchange_rows(needed, dom):
+    moved = [swapped(needed[k], "dom", k) for k in reversed(range(1, dom))]
+    return jnp.concatenate([needed[0]] + moved[::-1]), tuple(range(dom))
 
 
 def restore_kernel(plan, cut_ref, lane_restore, *refs):
@@ -475,7 +466,7 @@
         first = evolve(cutoffs, diffusion, courant, mats[:3], parts[: c + 1][-2:], order)
         addends = grid_sum(first, count, bits)
         needed = rows_for(dom, 1.0 / grids, addends)
-        home, sources = exchange_rows(*needed, dom)
+        home, sources = exchange_rows(needed, dom)
         held = [((0,), home[None])]
         for i in reversed(range(count)):
             for slots, piece in list(held):

time: 72.9 us -> 72.2 us (level)
  starting transfers between devices: 26.6 us -> 24.4 us
  waiting for transfers between devices: 31.9 us -> 33.5 us
    ppermute x10, starting transfers between devices: 12.5 us -> 9.7 us  [swapped_in_turn(): return lax.ppermute(x, ('grid', 'dom'), pairs)]
    ppermute x10, waiting for transfers between devices: 14.3 us -> 16.3 us  [swapped_in_turn(): return lax.ppermute(x, ('grid', 'dom'), pairs)]
    ppermute x12 -> x14, starting transfers between devices: 14.1 us -> 14.7 us  [swapped(): return lax.ppermute(x, axis, [(i, i ^ bit) for i in range(size)])]
    ppermute x12 -> x14, waiting for transfers between devices: 17.6 us -> 17.2 us  [swapped(): return lax.ppermute(x, axis, [(i, i ^ bit) for i in range(size)])]
  transfers between devices with their start and end apart: 22 -> 24, of which waited for: 14 -> 15; matrix products, arithmetic and copies ran while one was open for 0% -> 0% of each run, Pallas kernels for 7% -> 8%
where the time goes in v1:
time: 72.2 us; the launch traced here: 72.1 us
  waiting for transfers between devices  33.5 us (46%)
  starting transfers between devices  24.4 us (34%)
  Pallas kernels  12 us (17%)
  local copies, waits for them, and re-layouts  1.26 us (2%)
  between operations  0.79 us (1%)
    ppermute x14, waiting for transfers between devices, swapped(): return lax.ppermute(x, axis, [(i, i ^ bit) for i in range(size)])  17.2 us
    ppermute x10, waiting for transfers between devices, swapped_in_turn(): return lax.ppermute(x, ('grid', 'dom'), pairs)  16.3 us
    ppermute x14, starting transfers between devices, swapped(): return lax.ppermute(x, axis, [(i, i ^ bit) for i in range(size)])  14.7 us
    ppermute x10, starting transfers between devices, swapped_in_turn(): return lax.ppermute(x, ('grid', 'dom'), pairs)  9.7 us
    pallas_call x2, Pallas kernels, evolve(): pl.pallas_call(functools.partial(evolve_kernel, (dom, order, chunk, array...  7.39 us
    pallas_call x1, Pallas kernels, restore(): pl.pallas_call(functools.partial(restore_kernel, (dom, groups)), out_shap...  2.42 us
    pallas_call x1, Pallas kernels, tables(): pl.pallas_call(functools.partial(tables_kernel, (second_len, third_len)),...  1.7 us
  transfers between devices with their start and end apart: 24, of which 15 were waited for; matrix products, arithmetic and copies ran while one was open for 0% of the time, Pallas kernels for 8%

profile of v1, /device:TPU:0, one launch (start us, length us, event | category | flops | bytes accessed | tf_op | source)
XLA Modules:
  0.0 72.1 jit_solution(4030989833112273442)
XLA Ops:
  0.0 1.2 %copy-done = f32[1,4,16,16,256]{4,3,2,1,0:T(8,128)S(1)} copy-done((f32[1,4,16,16,256]{4,3,2,1,0:T(8,128)S(1)}, f32[1,4,16,16,256]{4,3,2,1,0:T(8,128)}, u32[]{:S(2)}) %copy-start) | copy-done | bytes 1048600
  1.2 0.5 shard_map.56
  1.7 0.6 collective-permute-start.12
  2.3 0.1 collective-permute-start
  2.3 2.9 %collective-permute-start.1 = (f32[4,48,256]{2,1,0:T(8,128)S(1)}, f32[4,48,256]{2,1,0:T(8,128)S(1)}, u32[]{:S(2)}, u32[]{:S(2)}) collective-permute-start(f32[4,48,256]{2,1,0:T(8,128)S(1)} %get-tuple-element.35), channel_id=1, source_target_pairs={{0,2},{1,3},{2,0},{3,1},{4,6},{5,7},{6,4},{7,5},{8,10},{9,11},{10,... | collective-permute-start | bytes 589832 | tf_op jit(solution)/shard_map/ppermute | solution.py:35
  5.2 0.0 collective-permute-start.2
  5.2 1.4 %collective-permute-start.13 = (f32[4,32,256]{2,1,0:T(8,128)S(1)}, f32[4,32,256]{2,1,0:T(8,128)S(1)}, u32[]{:S(2)}, u32[]{:S(2)}) collective-permute-start(f32[4,32,256]{2,1,0:T(8,128)S(1)} %get-tuple-element.45), channel_id=1, source_target_pairs={{0,2},{1,3},{2,0},{3,1},{4,6},{5,7},{6,4},{7,5},{8,10},{9,11},{10,... | collective-permute-start | bytes 393224 | tf_op jit(solution)/shard_map/ppermute | solution.py:35
  6.7 0.0 collective-permute-done.12.refs_5_
  6.7 0.4 collective-permute-start.14
  7.8 1.7 %shard_map.55 = (bf16[3,256,256]{2,1,0:T(8,128)(2,1)S(1)}, bf16[3,256,256]{2,1,0:T(8,128)(2,1)S(1)}, bf16[256,256]{1,0:T(8,128)(2,1)S(1)}, bf16[256,256]{1,0:T(8,128)(2,1)S(1)}) custom-call(s32[1,4]{1,0:T(1,128)S(1)} %copy-done.1, s32[1]{0:T(128)S(6)} %copy.6.weight_ref, f32[4]{0:T(128)S(1)} %copy-done.2, f32[4]{0:T(128)S(1)} %copy-done.3), custom_call_target="tpu_custom_call" | custom-call | tf_op jit(solution)/shard_map/pallas_call | solution.py:132
  9.5 8.5 %collective-permute-done.13.refs_6_ = f32[4,32,256]{2,1,0:T(8,128)S(1)} collective-permute-done((f32[4,32,256]{2,1,0:T(8,128)S(1)}, f32[4,32,256]{2,1,0:T(8,128)S(1)}, u32[]{:S(2)}, u32[]{:S(2)}) %collective-permute-start.13) | collective-permute-done | bytes 131104 | tf_op jit(solution)/shard_map/ppermute | solution.py:35
  18.0 1.6 %collective-permute-done.14.refs_7_ = f32[4,32,256]{2,1,0:T(8,128)S(1)} collective-permute-done((f32[4,32,256]{2,1,0:T(8,128)S(1)}, f32[4,32,256]{2,1,0:T(8,128)S(1)}, u32[]{:S(2)}, u32[]{:S(2)}) %collective-permute-start.14) | collective-permute-done | bytes 131104 | tf_op jit(solution)/shard_map/ppermute | solution.py:35
  19.6 0.0 collective-permute-done.refs_1_
  19.6 0.0 collective-permute-done.1.refs_2_
  19.6 0.0 collective-permute-done.2.refs_3_
  19.6 3.7 %shard_map.59 = (f32[2,16,8,256]{3,2,1,0:T(8,128)S(1)}, f32[2,16,8,256]{3,2,1,0:T(8,128)S(1)}) custom-call(s32[1,4]{1,0:T(1,128)S(1)} %copy-done.1, f32[4]{0:T(128)S(1)} %copy-done.2, f32[4]{0:T(128)S(1)} %copy-done.3, bf16[3,256,256]{2,1,0:T(8,128)(2,1)S(1)} %get-tuple-element.30.rate_high, bf16[3,256,256]{2,1,0:T(8,128)(2,1)S(1)} %get-tuple-element.31.rate_low, ...), custom_call_target="tpu_custom_call" | custom-call | tf_op jit(solution)/shard_map/pallas_call | solution.py:304
  23.3 1.6 %collective-permute-start.15 = (f32[2,16,8,256]{3,2,1,0:T(8,128)S(1)}, f32[2,16,8,256]{3,2,1,0:T(8,128)S(1)}, u32[]{:S(2)}, u32[]{:S(2)}) collective-permute-start(f32[2,16,8,256]{3,2,1,0:T(8,128)S(1)} %get-tuple-element.48), channel_id=1, source_target_pairs={{0,4},{1,9},{2,6},{3,11},{4,0},{5,13},{6,2},{7,15},{8,12},{9,1},{1... | collective-permute-start | bytes 786440 | tf_op jit(solution)/shard_map/ppermute | solution.py:48
  24.9 3.7 %shard_map.57 = (f32[2,16,8,256]{3,2,1,0:T(8,128)S(1)}, f32[2,16,8,256]{3,2,1,0:T(8,128)S(1)}) custom-call(s32[1,4]{1,0:T(1,128)S(1)} %copy-done.1, f32[4]{0:T(128)S(1)} %copy-done.2, f32[4]{0:T(128)S(1)} %copy-done.3, bf16[3,256,256]{2,1,0:T(8,128)(2,1)S(1)} %get-tuple-element.30.rate_high, bf16[3,256,256]{2,1,0:T(8,128)(2,1)S(1)} %get-tuple-element.31.rate_low, ...), custom_call_target="tpu_custom_call" | custom-call | tf_op jit(solution)/shard_map/pallas_call | solution.py:304
  28.6 0.6 collective-permute-start.3
  29.2 0.6 collective-permute-done.15
  29.8 1.6 %collective-permute-start.16 = (f32[1,16,8,256]{3,2,1,0:T(8,128)S(1)}, f32[1,16,8,256]{3,2,1,0:T(8,128)S(1)}, u32[]{:S(2)}, u32[]{:S(2)}) collective-permute-start(f32[1,16,8,256]{3,2,1,0:T(8,128)S(1)} %slice.19), channel_id=1, source_target_pairs={{0,8},{1,5},{2,10},{3,7},{4,12},{5,1},{6,14},{7,3},{8,0},{9,13},{1... | collective-permute-start | bytes 393224 | tf_op jit(solution)/shard_map/ppermute | solution.py:48
  31.4 4.9 %collective-permute-done.3 = f32[2,16,8,256]{3,2,1,0:T(8,128)S(1)} collective-permute-done((f32[2,16,8,256]{3,2,1,0:T(8,128)S(1)}, f32[2,16,8,256]{3,2,1,0:T(8,128)S(1)}, u32[]{:S(2)}, u32[]{:S(2)}) %collective-permute-start.3) | collective-permute-done | bytes 262176 | tf_op jit(solution)/shard_map/ppermute | solution.py:48
  36.4 1.7 %collective-permute-start.4 = (f32[1,16,8,256]{3,2,1,0:T(8,128)S(1)}, f32[1,16,8,256]{3,2,1,0:T(8,128)S(1)}, u32[]{:S(2)}, u32[]{:S(2)}) collective-permute-start(f32[1,16,8,256]{3,2,1,0:T(8,128)S(1)} %slice.17), channel_id=1, source_target_pairs={{0,8},{1,5},{2,10},{3,7},{4,12},{5,1},{6,14},{7,3},{8,0},{9,13},{1... | collective-permute-start | bytes 393224 | tf_op jit(solution)/shard_map/ppermute | solution.py:48
  38.2 2.6 %collective-permute-start.17 = (f32[16,8,256]{2,1,0:T(8,128)S(1)}, f32[16,8,256]{2,1,0:T(8,128)S(1)}, u32[]{:S(2)}, u32[]{:S(2)}) collective-permute-start(f32[16,8,256]{2,1,0:T(8,128)S(1)} %fusion.refs_0_), channel_id=1, source_target_pairs={{0,16},{4,20},{8,24},{12,28},{16,0},{20,4},{24,8},{28,12},{1,17},{... | collective-permute-start | bytes 393224 | tf_op jit(solution)/shard_map/ppermute | solution.py:35
  40.8 1.8 %collective-permute-done.4 = f32[1,16,8,256]{3,2,1,0:T(8,128)S(1)} collective-permute-done((f32[1,16,8,256]{3,2,1,0:T(8,128)S(1)}, f32[1,16,8,256]{3,2,1,0:T(8,128)S(1)}, u32[]{:S(2)}, u32[]{:S(2)}) %collective-permute-start.4) | collective-permute-done | bytes 131104 | tf_op jit(solution)/shard_map/ppermute | solution.py:48
  42.7 2.8 %collective-permute-start.5 = (f32[16,8,256]{2,1,0:T(8,128)S(1)}, f32[16,8,256]{2,1,0:T(8,128)S(1)}, u32[]{:S(2)}, u32[]{:S(2)}) collective-permute-start(f32[16,8,256]{2,1,0:T(8,128)S(1)} %fusion.1.refs_0_), channel_id=1, source_target_pairs={{0,16},{4,20},{8,24},{12,28},{16,0},{20,4},{24,8},{28,12},{1,17},{... | collective-permute-start | bytes 393224 | tf_op jit(solution)/shard_map/ppermute | solution.py:35
  45.5 4.0 %collective-permute-done.17.refs_1_ = f32[16,8,256]{2,1,0:T(8,128)S(1)} collective-permute-done((f32[16,8,256]{2,1,0:T(8,128)S(1)}, f32[16,8,256]{2,1,0:T(8,128)S(1)}, u32[]{:S(2)}, u32[]{:S(2)}) %collective-permute-start.17) | collective-permute-done | bytes 131104 | tf_op jit(solution)/shard_map/ppermute | solution.py:35
  49.5 0.1 collective-permute-start.18
  49.6 1.6 %collective-permute-start.19 = (f32[1,5,8,256]{3,2,1,0:T(8,128)S(1)}, f32[1,5,8,256]{3,2,1,0:T(8,128)S(1)}, u32[]{:S(2)}, u32[]{:S(2)}) collective-permute-start(f32[1,5,8,256]{3,2,1,0:T(8,128)S(1)} %get-tuple-element.51), channel_id=1, source_target_pairs={{0,2},{1,3},{2,0},{3,1},{4,6},{5,7},{6,4},{7,5},{8,10},{9,11},{10,... | collective-permute-start | bytes 122888 | tf_op jit(solution)/shard_map/ppermute | solution.py:35
  51.1 0.3 collective-permute-start.20
  51.5 0.4 collective-permute-start.6
  51.9 1.5 %collective-permute-start.7 = (f32[1,5,8,256]{3,2,1,0:T(8,128)S(1)}, f32[1,5,8,256]{3,2,1,0:T(8,128)S(1)}, u32[]{:S(2)}, u32[]{:S(2)}) collective-permute-start(f32[1,5,8,256]{3,2,1,0:T(8,128)S(1)} %get-tuple-element.41), channel_id=1, source_target_pairs={{0,2},{1,3},{2,0},{3,1},{4,6},{5,7},{6,4},{7,5},{8,10},{9,11},{10,... | collective-permute-start | bytes 122888 | tf_op jit(solution)/shard_map/ppermute | solution.py:35
  53.4 0.0 collective-permute-start.8
  53.4 0.3 collective-permute-done.19
  53.7 1.0 %collective-permute-done.20 = f32[1,5,8,256]{3,2,1,0:T(8,128)S(1)} collective-permute-done((f32[1,5,8,256]{3,2,1,0:T(8,128)S(1)}, f32[1,5,8,256]{3,2,1,0:T(8,128)S(1)}, u32[]{:S(2)}, u32[]{:S(2)}) %collective-permute-start.20) | collective-permute-done | bytes 40992 | tf_op jit(solution)/shard_map/ppermute | solution.py:35
  54.7 0.7 %collective-permute-start.21 = (f32[1,4,5,8,256]{4,3,2,1,0:T(8,128)S(1)}, f32[1,4,5,8,256]{4,3,2,1,0:T(8,128)S(1)}, u32[]{:S(2)}, u32[]{:S(2)}) collective-permute-start(f32[1,4,5,8,256]{4,3,2,1,0:T(8,128)S(1)} %maximum_bitcast_fusion.1.refs_4_), channel_id=1, source_target_pairs={{0,8},{1,5},{2,10},{3,7},{4,12},{5,1},{6,14},{7,3},{8,0},{9,13},{1... | collective-permute-start | bytes 491528 | tf_op jit(solution)/shard_map/ppermute | solution.py:48
  55.4 0.5 collective-permute-done.7
  55.9 1.3 %collective-permute-done.8 = f32[1,5,8,256]{3,2,1,0:T(8,128)S(1)} collective-permute-done((f32[1,5,8,256]{3,2,1,0:T(8,128)S(1)}, f32[1,5,8,256]{3,2,1,0:T(8,128)S(1)}, u32[]{:S(2)}, u32[]{:S(2)}) %collective-permute-start.8) | collective-permute-done | bytes 40992 | tf_op jit(solution)/shard_map/ppermute | solution.py:35
  57.2 0.7 %collective-permute-start.9 = (f32[1,4,5,8,256]{4,3,2,1,0:T(8,128)S(1)}, f32[1,4,5,8,256]{4,3,2,1,0:T(8,128)S(1)}, u32[]{:S(2)}, u32[]{:S(2)}) collective-permute-start(f32[1,4,5,8,256]{4,3,2,1,0:T(8,128)S(1)} %maximum_bitcast_fusion.refs_0_), channel_id=1, source_target_pairs={{0,8},{1,5},{2,10},{3,7},{4,12},{5,1},{6,14},{7,3},{8,0},{9,13},{1... | collective-permute-start | bytes 491528 | tf_op jit(solution)/shard_map/ppermute | solution.py:48
  57.9 0.6 collective-permute-start.22
  58.6 1.4 %collective-permute-start.10 = (f32[1,4,5,8,256]{4,3,2,1,0:T(8,128)S(1)}, f32[1,4,5,8,256]{4,3,2,1,0:T(8,128)S(1)}, u32[]{:S(2)}, u32[]{:S(2)}) collective-permute-start(f32[1,4,5,8,256]{4,3,2,1,0:T(8,128)S(1)} %maximum_bitcast_fusion.refs_0_), channel_id=1, source_target_pairs={{0,4},{1,9},{2,6},{3,11},{4,0},{5,13},{6,2},{7,15},{8,12},{9,1},{1... | collective-permute-start | bytes 491528 | tf_op jit(solution)/shard_map/ppermute | solution.py:48
  60.0 0.1 collective-permute-done.21.refs_5_
  60.1 0.7 %collective-permute-start.23 = (f32[1,4,5,8,256]{4,3,2,1,0:T(8,128)S(1)}, f32[1,4,5,8,256]{4,3,2,1,0:T(8,128)S(1)}, u32[]{:S(2)}, u32[]{:S(2)}) collective-permute-start(f32[1,4,5,8,256]{4,3,2,1,0:T(8,128)S(1)} %collective-permute-done.21.refs_5_), channel_id=1, source_target_pairs={{0,4},{1,9},{2,6},{3,11},{4,0},{5,13},{6,2},{7,15},{8,12},{9,1},{1... | collective-permute-start | bytes 491528 | tf_op jit(solution)/shard_map/ppermute | solution.py:48
  60.8 3.5 %collective-permute-done.9.refs_1_ = f32[1,4,5,8,256]{4,3,2,1,0:T(8,128)S(1)} collective-permute-done((f32[1,4,5,8,256]{4,3,2,1,0:T(8,128)S(1)}, f32[1,4,5,8,256]{4,3,2,1,0:T(8,128)S(1)}, u32[]{:S(2)}, u32[]{:S(2)}) %collective-permute-start.9) | collective-permute-done | bytes 163872 | tf_op jit(solution)/shard_map/ppermute | solution.py:48
  64.4 0.9 %collective-permute-done.10.refs_2_ = f32[1,4,5,8,256]{4,3,2,1,0:T(8,128)S(1)} collective-permute-done((f32[1,4,5,8,256]{4,3,2,1,0:T(8,128)S(1)}, f32[1,4,5,8,256]{4,3,2,1,0:T(8,128)S(1)}, u32[]{:S(2)}, u32[]{:S(2)}) %collective-permute-start.10) | collective-permute-done | bytes 163872 | tf_op jit(solution)/shard_map/ppermute | solution.py:48
  65.3 1.8 %collective-permute-done.23.refs_7_ = f32[1,4,5,8,256]{4,3,2,1,0:T(8,128)S(1)} collective-permute-done((f32[1,4,5,8,256]{4,3,2,1,0:T(8,128)S(1)}, f32[1,4,5,8,256]{4,3,2,1,0:T(8,128)S(1)}, u32[]{:S(2)}, u32[]{:S(2)}) %collective-permute-start.23) | collective-permute-done | bytes 163872 | tf_op jit(solution)/shard_map/ppermute | solution.py:48
  67.0 2.7 %collective-permute-done.11.refs_3_ = f32[1,4,5,8,256]{4,3,2,1,0:T(8,128)S(1)} collective-permute-done((f32[1,4,5,8,256]{4,3,2,1,0:T(8,128)S(1)}, f32[1,4,5,8,256]{4,3,2,1,0:T(8,128)S(1)}, u32[]{:S(2)}, u32[]{:S(2)}) %collective-permute-start.11) | collective-permute-done | bytes 163872 | tf_op jit(solution)/shard_map/ppermute | solution.py:48
  69.7 2.4 %shard_map.61 = f32[4,256,256]{2,1,0:T(8,128)} custom-call(s32[1,4]{1,0:T(1,128)S(1)} %copy-done.1, bf16[256,256]{1,0:T(8,128)(2,1)S(1)} %get-tuple-element.29.lane_restore, f32[1,4,5,8,256]{4,3,2,1,0:T(8,128)S(1)} %maximum_bitcast_fusion.refs_0_, f32[1,4,5,8,256]{4,3,2,1,0:T(8,128)S(1)} %collective-permute-done.9.refs_1_, ...), custom_call_target="tpu_custom_call" | custom-call | tf_op jit(solution)/shard_map/pallas_call | solution.py:410
  (23 shorter events, 0.2 us)
Async XLA Ops:
  0.0 1.2 %copy-start = (f32[1,4,16,16,256]{4,3,2,1,0:T(8,128)S(1)}, f32[1,4,16,16,256]{4,3,2,1,0:T(8,128)}, u32[]{:S(2)}) copy-start(f32[1,4,16,16,256]{4,3,2,1,0:T(8,128)} %param.5) | copy-start | bytes 3145732
  1.7 5.0 %collective-permute-start.12 = (f32[4,32,256]{2,1,0:T(8,128)S(1)}, f32[4,32,256]{2,1,0:T(8,128)S(1)}, u32[]{:S(2)}, u32[]{:S(2)}) collective-permute-start(f32[4,32,256]{2,1,0:T(8,128)S(1)} %get-tuple-element.44), channel_id=1, source_target_pairs={{0,1},{1,0},{2,3},{3,2},{4,5},{5,4},{6,7},{7,6},{8,9},{9,8},{10,11... | collective-permute-start | bytes 393224 | tf_op jit(solution)/shard_map/ppermute | solution.py:35
  2.3 17.3 %collective-permute-start = (f32[4,48,256]{2,1,0:T(8,128)S(1)}, f32[4,48,256]{2,1,0:T(8,128)S(1)}, u32[]{:S(2)}, u32[]{:S(2)}) collective-permute-start(f32[4,48,256]{2,1,0:T(8,128)S(1)} %get-tuple-element.34), channel_id=1, source_target_pairs={{0,1},{1,0},{2,3},{3,2},{4,5},{5,4},{6,7},{7,6},{8,9},{9,8},{10,11... | collective-permute-start | bytes 589832 | tf_op jit(solution)/shard_map/ppermute | solution.py:35
  2.3 17.3 %collective-permute-start.1 = (f32[4,48,256]{2,1,0:T(8,128)S(1)}, f32[4,48,256]{2,1,0:T(8,128)S(1)}, u32[]{:S(2)}, u32[]{:S(2)}) collective-permute-start(f32[4,48,256]{2,1,0:T(8,128)S(1)} %get-tuple-element.35), channel_id=1, source_target_pairs={{0,2},{1,3},{2,0},{3,1},{4,6},{5,7},{6,4},{7,5},{8,10},{9,11},{10,... | collective-permute-start | bytes 589832 | tf_op jit(solution)/shard_map/ppermute | solution.py:35
  5.2 14.4 %collective-permute-start.2 = (f32[4,48,256]{2,1,0:T(8,128)S(1)}, f32[4,48,256]{2,1,0:T(8,128)S(1)}, u32[]{:S(2)}, u32[]{:S(2)}) collective-permute-start(f32[4,48,256]{2,1,0:T(8,128)S(1)} %get-tuple-element.36), channel_id=1, source_target_pairs={{0,3},{1,2},{2,1},{3,0},{4,7},{5,6},{6,5},{7,4},{8,11},{9,10},{10,... | collective-permute-start | bytes 589832 | tf_op jit(solution)/shard_map/ppermute | solution.py:35
  5.2 12.8 %collective-permute-start.13 = (f32[4,32,256]{2,1,0:T(8,128)S(1)}, f32[4,32,256]{2,1,0:T(8,128)S(1)}, u32[]{:S(2)}, u32[]{:S(2)}) collective-permute-start(f32[4,32,256]{2,1,0:T(8,128)S(1)} %get-tuple-element.45), channel_id=1, source_target_pairs={{0,2},{1,3},{2,0},{3,1},{4,6},{5,7},{6,4},{7,5},{8,10},{9,11},{10,... | collective-permute-start | bytes 393224 | tf_op jit(solution)/shard_map/ppermute | solution.py:35
  6.7 1.1 %copy-start.1 = (s32[1,4]{1,0:T(1,128)S(1)}, s32[1,4]{1,0:T(1,128)}, u32[]{:S(2)}) copy-start(s32[1,4]{1,0:T(1,128)} %cut_ref.7) | copy-start | bytes 52
  6.7 1.1 %copy-start.2 = (f32[4]{0:T(128)S(1)}, f32[4]{0:T(128)}, u32[]{:S(2)}) copy-start(f32[4]{0:T(128)} %diff_ref.5) | copy-start | bytes 52
  6.7 1.1 %copy-start.3 = (f32[4]{0:T(128)S(1)}, f32[4]{0:T(128)}, u32[]{:S(2)}) copy-start(f32[4]{0:T(128)} %cour_ref.5) | copy-start | bytes 52
  6.7 12.9 %collective-permute-start.14 = (f32[4,32,256]{2,1,0:T(8,128)S(1)}, f32[4,32,256]{2,1,0:T(8,128)S(1)}, u32[]{:S(2)}, u32[]{:S(2)}) collective-permute-start(f32[4,32,256]{2,1,0:T(8,128)S(1)} %get-tuple-element.46), channel_id=1, source_target_pairs={{0,3},{1,2},{2,1},{3,0},{4,7},{5,6},{6,5},{7,4},{8,11},{9,10},{10,... | collective-permute-start | bytes 393224 | tf_op jit(solution)/shard_map/ppermute | solution.py:35
  23.3 6.4 %collective-permute-start.15 = (f32[2,16,8,256]{3,2,1,0:T(8,128)S(1)}, f32[2,16,8,256]{3,2,1,0:T(8,128)S(1)}, u32[]{:S(2)}, u32[]{:S(2)}) collective-permute-start(f32[2,16,8,256]{3,2,1,0:T(8,128)S(1)} %get-tuple-element.48), channel_id=1, source_target_pairs={{0,4},{1,9},{2,6},{3,11},{4,0},{5,13},{6,2},{7,15},{8,12},{9,1},{1... | collective-permute-start | bytes 786440 | tf_op jit(solution)/shard_map/ppermute | solution.py:48
  28.6 7.8 %collective-permute-start.3 = (f32[2,16,8,256]{3,2,1,0:T(8,128)S(1)}, f32[2,16,8,256]{3,2,1,0:T(8,128)S(1)}, u32[]{:S(2)}, u32[]{:S(2)}) collective-permute-start(f32[2,16,8,256]{3,2,1,0:T(8,128)S(1)} %get-tuple-element.38), channel_id=1, source_target_pairs={{0,4},{1,9},{2,6},{3,11},{4,0},{5,13},{6,2},{7,15},{8,12},{9,1},{1... | collective-permute-start | bytes 786440 | tf_op jit(solution)/shard_map/ppermute | solution.py:48
  29.8 8.3 %collective-permute-start.16 = (f32[1,16,8,256]{3,2,1,0:T(8,128)S(1)}, f32[1,16,8,256]{3,2,1,0:T(8,128)S(1)}, u32[]{:S(2)}, u32[]{:S(2)}) collective-permute-start(f32[1,16,8,256]{3,2,1,0:T(8,128)S(1)} %slice.19), channel_id=1, source_target_pairs={{0,8},{1,5},{2,10},{3,7},{4,12},{5,1},{6,14},{7,3},{8,0},{9,13},{1... | collective-permute-start | bytes 393224 | tf_op jit(solution)/shard_map/ppermute | solution.py:48
  36.4 6.2 %collective-permute-start.4 = (f32[1,16,8,256]{3,2,1,0:T(8,128)S(1)}, f32[1,16,8,256]{3,2,1,0:T(8,128)S(1)}, u32[]{:S(2)}, u32[]{:S(2)}) collective-permute-start(f32[1,16,8,256]{3,2,1,0:T(8,128)S(1)} %slice.17), channel_id=1, source_target_pairs={{0,8},{1,5},{2,10},{3,7},{4,12},{5,1},{6,14},{7,3},{8,0},{9,13},{1... | collective-permute-start | bytes 393224 | tf_op jit(solution)/shard_map/ppermute | solution.py:48
  38.2 11.3 %collective-permute-start.17 = (f32[16,8,256]{2,1,0:T(8,128)S(1)}, f32[16,8,256]{2,1,0:T(8,128)S(1)}, u32[]{:S(2)}, u32[]{:S(2)}) collective-permute-start(f32[16,8,256]{2,1,0:T(8,128)S(1)} %fusion.refs_0_), channel_id=1, source_target_pairs={{0,16},{4,20},{8,24},{12,28},{16,0},{20,4},{24,8},{28,12},{1,17},{... | collective-permute-start | bytes 393224 | tf_op jit(solution)/shard_map/ppermute | solution.py:35
  42.7 8.8 %collective-permute-start.5 = (f32[16,8,256]{2,1,0:T(8,128)S(1)}, f32[16,8,256]{2,1,0:T(8,128)S(1)}, u32[]{:S(2)}, u32[]{:S(2)}) collective-permute-start(f32[16,8,256]{2,1,0:T(8,128)S(1)} %fusion.1.refs_0_), channel_id=1, source_target_pairs={{0,16},{4,20},{8,24},{12,28},{16,0},{20,4},{24,8},{28,12},{1,17},{... | collective-permute-start | bytes 393224 | tf_op jit(solution)/shard_map/ppermute | solution.py:35
  49.5 3.9 %collective-permute-start.18 = (f32[1,5,8,256]{3,2,1,0:T(8,128)S(1)}, f32[1,5,8,256]{3,2,1,0:T(8,128)S(1)}, u32[]{:S(2)}, u32[]{:S(2)}) collective-permute-start(f32[1,5,8,256]{3,2,1,0:T(8,128)S(1)} %get-tuple-element.50), channel_id=1, source_target_pairs={{0,1},{1,0},{2,3},{3,2},{4,5},{5,4},{6,7},{7,6},{8,9},{9,8},{10,11... | collective-permute-start | bytes 122888 | tf_op jit(solution)/shard_map/ppermute | solution.py:35
  49.6 4.1 %collective-permute-start.19 = (f32[1,5,8,256]{3,2,1,0:T(8,128)S(1)}, f32[1,5,8,256]{3,2,1,0:T(8,128)S(1)}, u32[]{:S(2)}, u32[]{:S(2)}) collective-permute-start(f32[1,5,8,256]{3,2,1,0:T(8,128)S(1)} %get-tuple-element.51), channel_id=1, source_target_pairs={{0,2},{1,3},{2,0},{3,1},{4,6},{5,7},{6,4},{7,5},{8,10},{9,11},{10,... | collective-permute-start | bytes 122888 | tf_op jit(solution)/shard_map/ppermute | solution.py:35
  51.1 3.5 %collective-permute-start.20 = (f32[1,5,8,256]{3,2,1,0:T(8,128)S(1)}, f32[1,5,8,256]{3,2,1,0:T(8,128)S(1)}, u32[]{:S(2)}, u32[]{:S(2)}) collective-permute-start(f32[1,5,8,256]{3,2,1,0:T(8,128)S(1)} %get-tuple-element.52), channel_id=1, source_target_pairs={{0,3},{1,2},{2,1},{3,0},{4,7},{5,6},{6,5},{7,4},{8,11},{9,10},{10,... | collective-permute-start | bytes 122888 | tf_op jit(solution)/shard_map/ppermute | solution.py:35
  51.5 4.0 %collective-permute-start.6 = (f32[1,5,8,256]{3,2,1,0:T(8,128)S(1)}, f32[1,5,8,256]{3,2,1,0:T(8,128)S(1)}, u32[]{:S(2)}, u32[]{:S(2)}) collective-permute-start(f32[1,5,8,256]{3,2,1,0:T(8,128)S(1)} %get-tuple-element.40), channel_id=1, source_target_pairs={{0,1},{1,0},{2,3},{3,2},{4,5},{5,4},{6,7},{7,6},{8,9},{9,8},{10,11... | collective-permute-start | bytes 122888 | tf_op jit(solution)/shard_map/ppermute | solution.py:35
  51.9 4.0 %collective-permute-start.7 = (f32[1,5,8,256]{3,2,1,0:T(8,128)S(1)}, f32[1,5,8,256]{3,2,1,0:T(8,128)S(1)}, u32[]{:S(2)}, u32[]{:S(2)}) collective-permute-start(f32[1,5,8,256]{3,2,1,0:T(8,128)S(1)} %get-tuple-element.41), channel_id=1, source_target_pairs={{0,2},{1,3},{2,0},{3,1},{4,6},{5,7},{6,4},{7,5},{8,10},{9,11},{10,... | collective-permute-start | bytes 122888 | tf_op jit(solution)/shard_map/ppermute | solution.py:35
  53.4 3.8 %collective-permute-start.8 = (f32[1,5,8,256]{3,2,1,0:T(8,128)S(1)}, f32[1,5,8,256]{3,2,1,0:T(8,128)S(1)}, u32[]{:S(2)}, u32[]{:S(2)}) collective-permute-start(f32[1,5,8,256]{3,2,1,0:T(8,128)S(1)} %get-tuple-element.42), channel_id=1, source_target_pairs={{0,3},{1,2},{2,1},{3,0},{4,7},{5,6},{6,5},{7,4},{8,11},{9,10},{10,... | collective-permute-start | bytes 122888 | tf_op jit(solution)/shard_map/ppermute | solution.py:35
  54.7 5.4 %collective-permute-start.21 = (f32[1,4,5,8,256]{4,3,2,1,0:T(8,128)S(1)}, f32[1,4,5,8,256]{4,3,2,1,0:T(8,128)S(1)}, u32[]{:S(2)}, u32[]{:S(2)}) collective-permute-start(f32[1,4,5,8,256]{4,3,2,1,0:T(8,128)S(1)} %maximum_bitcast_fusion.1.refs_4_), channel_id=1, source_target_pairs={{0,8},{1,5},{2,10},{3,7},{4,12},{5,1},{6,14},{7,3},{8,0},{9,13},{1... | collective-permute-start | bytes 491528 | tf_op jit(solution)/shard_map/ppermute | solution.py:48
  57.2 7.1 %collective-permute-start.9 = (f32[1,4,5,8,256]{4,3,2,1,0:T(8,128)S(1)}, f32[1,4,5,8,256]{4,3,2,1,0:T(8,128)S(1)}, u32[]{:S(2)}, u32[]{:S(2)}) collective-permute-start(f32[1,4,5,8,256]{4,3,2,1,0:T(8,128)S(1)} %maximum_bitcast_fusion.refs_0_), channel_id=1, source_target_pairs={{0,8},{1,5},{2,10},{3,7},{4,12},{5,1},{6,14},{7,3},{8,0},{9,13},{1... | collective-permute-start | bytes 491528 | tf_op jit(solution)/shard_map/ppermute | solution.py:48
  57.9 6.4 %collective-permute-start.22 = (f32[1,4,5,8,256]{4,3,2,1,0:T(8,128)S(1)}, f32[1,4,5,8,256]{4,3,2,1,0:T(8,128)S(1)}, u32[]{:S(2)}, u32[]{:S(2)}) collective-permute-start(f32[1,4,5,8,256]{4,3,2,1,0:T(8,128)S(1)} %maximum_bitcast_fusion.1.refs_4_), channel_id=1, source_target_pairs={{0,4},{1,9},{2,6},{3,11},{4,0},{5,13},{6,2},{7,15},{8,12},{9,1},{1... | collective-permute-start | bytes 491528 | tf_op jit(solution)/shard_map/ppermute | solution.py:48
  58.6 6.7 %collective-permute-start.10 = (f32[1,4,5,8,256]{4,3,2,1,0:T(8,128)S(1)}, f32[1,4,5,8,256]{4,3,2,1,0:T(8,128)S(1)}, u32[]{:S(2)}, u32[]{:S(2)}) collective-permute-start(f32[1,4,5,8,256]{4,3,2,1,0:T(8,128)S(1)} %maximum_bitcast_fusion.refs_0_), channel_id=1, source_target_pairs={{0,4},{1,9},{2,6},{3,11},{4,0},{5,13},{6,2},{7,15},{8,12},{9,1},{1... | collective-permute-start | bytes 491528 | tf_op jit(solution)/shard_map/ppermute | solution.py:48
  60.1 6.9 %collective-permute-start.23 = (f32[1,4,5,8,256]{4,3,2,1,0:T(8,128)S(1)}, f32[1,4,5,8,256]{4,3,2,1,0:T(8,128)S(1)}, u32[]{:S(2)}, u32[]{:S(2)}) collective-permute-start(f32[1,4,5,8,256]{4,3,2,1,0:T(8,128)S(1)} %collective-permute-done.21.refs_5_), channel_id=1, source_target_pairs={{0,4},{1,9},{2,6},{3,11},{4,0},{5,13},{6,2},{7,15},{8,12},{9,1},{1... | collective-permute-start | bytes 491528 | tf_op jit(solution)/shard_map/ppermute | solution.py:48
  64.3 5.3 %collective-permute-start.11 = (f32[1,4,5,8,256]{4,3,2,1,0:T(8,128)S(1)}, f32[1,4,5,8,256]{4,3,2,1,0:T(8,128)S(1)}, u32[]{:S(2)}, u32[]{:S(2)}) collective-permute-start(f32[1,4,5,8,256]{4,3,2,1,0:T(8,128)S(1)} %collective-permute-done.9.refs_1_), channel_id=1, source_target_pairs={{0,4},{1,9},{2,6},{3,11},{4,0},{5,13},{6,2},{7,15},{8,12},{9,1},{1... | collective-permute-start | bytes 491528 | tf_op jit(solution)/shard_map/ppermute | solution.py:48

commit v2 on v1

--- a/solution.py
+++ b/solution.py
@@ -13,7 +13,7 @@
 TILE = 8
 LANES = 128
 GROUP = 16
-EAGER = "ab"
+SPLIT = "b"
 CHAINS = 2
 
 VMEM = pl.BlockSpec(memory_space=pltpu.VMEM)
@@ -344,7 +344,7 @@
 
 def exchange_rows(needed, dom):
     moved = [swapped(needed[k], "dom", k) for k in reversed(range(1, dom))]
-    return jnp.concatenate([needed[0]] + moved[::-1]), tuple(range(dom))
+    return [needed[0]] + moved[::-1]
 
 
 def restore_kernel(plan, cut_ref, lane_restore, *refs):
@@ -466,18 +466,20 @@
         first = evolve(cutoffs, diffusion, courant, mats[:3], parts[: c + 1][-2:], order)
         addends = grid_sum(first, count, bits)
         needed = rows_for(dom, 1.0 / grids, addends)
-        home, sources = exchange_rows(needed, dom)
-        held = [((0,), home[None])]
-        for i in reversed(range(count)):
-            for slots, piece in list(held):
-                arrived = swapped_in_turn(piece, i, count)
-                held.append((tuple(q | 1 << i for q in slots), arrived))
-            if i and chain not in EAGER:
-                slots = sum((slots for slots, _ in held), ())
-                held = [(slots, jnp.concatenate([piece for _, piece in held]))]
-        for slots, piece in held:
-            arrays.append(piece)
-            groups.append((c, count, slots, sources))
+        home, sources = exchange_rows(needed, dom), tuple(range(dom))
+        parts_home = [(home, sources)]
+        if chain in SPLIT:
+            half = len(sources) // 2
+            parts_home = [(home[:half], sources[:half]), (home[half:], sources[half:])]
+        for some, places in parts_home:
+            held = [((0,), jnp.concatenate(some)[None])]
+            for i in reversed(range(count)):
+                for slots, piece in list(held):
+                    arrived = swapped_in_turn(piece, i, count)
+                    held.append((tuple(q | 1 << i for q in slots), arrived))
+            for slots, piece in held:
+                arrays.append(piece)
+                groups.append((c, count, slots, places))
     out = restore(cutoffs, mats[3], arrays, tuple(groups), dom, rows, lanes, length)
     return out.reshape(1, rows, second_len, third_len, length)
 

time: 72.2 us -> 67.8 us (0.939)
  waiting for transfers between devices: 33.5 us -> 24.1 us
  starting transfers between devices: 24.4 us -> 29.4 us
    ppermute x10 -> x13, waiting for transfers between devices: 16.3 us -> 10.4 us  [swapped_in_turn(): return lax.ppermute(x, ('grid', 'dom'), pairs)]
    ppermute x10 -> x13, starting transfers between devices: 9.7 us -> 14.8 us  [swapped_in_turn(): return lax.ppermute(x, ('grid', 'dom'), pairs)]
    ppermute x14, waiting for transfers between devices: 17.2 us -> 13.7 us  [swapped(): return lax.ppermute(x, axis, [(i, i ^ bit) for i in range(size)])]
  transfers between devices with their start and end apart: 24 -> 27, of which waited for: 15 -> 15; matrix products, arithmetic and copies ran while one was open for 0% -> 0% of each run, Pallas kernels for 8% -> 13%
where the time goes in v2:
time: 67.8 us; the launch traced here: 67.7 us
  starting transfers between devices  29.4 us (43%)
  waiting for transfers between devices  24.1 us (36%)
  Pallas kernels  12 us (18%)
  local copies, waits for them, and re-layouts  1.26 us (2%)
  between operations  0.81 us (1%)
    ppermute x13, starting transfers between devices, swapped_in_turn(): return lax.ppermute(x, ('grid', 'dom'), pairs)  14.8 us
    ppermute x14, starting transfers between devices, swapped(): return lax.ppermute(x, axis, [(i, i ^ bit) for i in range(size)])  14.6 us
    ppermute x14, waiting for transfers between devices, swapped(): return lax.ppermute(x, axis, [(i, i ^ bit) for i in range(size)])  13.7 us
    ppermute x13, waiting for transfers between devices, swapped_in_turn(): return lax.ppermute(x, ('grid', 'dom'), pairs)  10.4 us
    pallas_call x2, Pallas kernels, evolve(): pl.pallas_call(functools.partial(evolve_kernel, (dom, order, chunk, array...  7.39 us
    pallas_call x1, Pallas kernels, restore(): pl.pallas_call(functools.partial(restore_kernel, (dom, groups)), out_shap...  2.43 us
    pallas_call x1, Pallas kernels, tables(): pl.pallas_call(functools.partial(tables_kernel, (second_len, third_len)),...  1.7 us
  transfers between devices with their start and end apart: 27, of which 15 were waited for; matrix products, arithmetic and copies ran while one was open for 0% of the time, Pallas kernels for 13%

profile of v2, /device:TPU:0, one launch (start us, length us, event | category | flops | bytes accessed | tf_op | source)
XLA Modules:
  0.0 67.7 jit_solution(11555489205588374820)
XLA Ops:
  0.0 1.2 %copy-done = f32[1,4,16,16,256]{4,3,2,1,0:T(8,128)S(1)} copy-done((f32[1,4,16,16,256]{4,3,2,1,0:T(8,128)S(1)}, f32[1,4,16,16,256]{4,3,2,1,0:T(8,128)}, u32[]{:S(2)}) %copy-start) | copy-done | bytes 1048600
  1.2 0.5 shard_map.56
  1.7 0.6 collective-permute-start
  2.3 2.5 %collective-permute-start.1 = (f32[4,48,256]{2,1,0:T(8,128)S(1)}, f32[4,48,256]{2,1,0:T(8,128)S(1)}, u32[]{:S(2)}, u32[]{:S(2)}) collective-permute-start(f32[4,48,256]{2,1,0:T(8,128)S(1)} %get-tuple-element.35), channel_id=1, source_target_pairs={{0,2},{1,3},{2,0},{3,1},{4,6},{5,7},{6,4},{7,5},{8,10},{9,11},{10,... | collective-permute-start | bytes 589832 | tf_op jit(solution)/shard_map/ppermute | solution.py:35
  4.8 0.0 collective-permute-start.2
  4.8 0.2 collective-permute-start.12
  5.0 1.9 %collective-permute-start.13 = (f32[4,32,256]{2,1,0:T(8,128)S(1)}, f32[4,32,256]{2,1,0:T(8,128)S(1)}, u32[]{:S(2)}, u32[]{:S(2)}) collective-permute-start(f32[4,32,256]{2,1,0:T(8,128)S(1)} %get-tuple-element.45), channel_id=1, source_target_pairs={{0,2},{1,3},{2,0},{3,1},{4,6},{5,7},{6,4},{7,5},{8,10},{9,11},{10,... | collective-permute-start | bytes 393224 | tf_op jit(solution)/shard_map/ppermute | solution.py:35
  7.6 1.7 %shard_map.55 = (bf16[3,256,256]{2,1,0:T(8,128)(2,1)S(1)}, bf16[3,256,256]{2,1,0:T(8,128)(2,1)S(1)}, bf16[256,256]{1,0:T(8,128)(2,1)S(1)}, bf16[256,256]{1,0:T(8,128)(2,1)S(1)}) custom-call(s32[1,4]{1,0:T(1,128)S(1)} %copy-done.1, s32[1]{0:T(128)S(6)} %copy.6.weight_ref, f32[4]{0:T(128)S(1)} %copy-done.2, f32[4]{0:T(128)S(1)} %copy-done.3), custom_call_target="tpu_custom_call" | custom-call | tf_op jit(solution)/shard_map/pallas_call | solution.py:132
  9.3 0.1 collective-permute-start.14
  9.4 1.1 %collective-permute-done.1.refs_2_ = f32[4,48,256]{2,1,0:T(8,128)S(1)} collective-permute-done((f32[4,48,256]{2,1,0:T(8,128)S(1)}, f32[4,48,256]{2,1,0:T(8,128)S(1)}, u32[]{:S(2)}, u32[]{:S(2)}) %collective-permute-start.1) | collective-permute-done | bytes 196640 | tf_op jit(solution)/shard_map/ppermute | solution.py:35
  10.6 3.8 %collective-permute-done.2.refs_3_ = f32[4,48,256]{2,1,0:T(8,128)S(1)} collective-permute-done((f32[4,48,256]{2,1,0:T(8,128)S(1)}, f32[4,48,256]{2,1,0:T(8,128)S(1)}, u32[]{:S(2)}, u32[]{:S(2)}) %collective-permute-start.2) | collective-permute-done | bytes 196640 | tf_op jit(solution)/shard_map/ppermute | solution.py:35
  14.3 3.7 %shard_map.57 = (f32[2,16,8,256]{3,2,1,0:T(8,128)S(1)}, f32[2,16,8,256]{3,2,1,0:T(8,128)S(1)}) custom-call(s32[1,4]{1,0:T(1,128)S(1)} %copy-done.1, f32[4]{0:T(128)S(1)} %copy-done.2, f32[4]{0:T(128)S(1)} %copy-done.3, bf16[3,256,256]{2,1,0:T(8,128)(2,1)S(1)} %get-tuple-element.30.rate_high, bf16[3,256,256]{2,1,0:T(8,128)(2,1)S(1)} %get-tuple-element.31.rate_low, ...), custom_call_target="tpu_custom_call" | custom-call | tf_op jit(solution)/shard_map/pallas_call | solution.py:304
  18.0 1.6 %collective-permute-start.3 = (f32[2,16,8,256]{3,2,1,0:T(8,128)S(1)}, f32[2,16,8,256]{3,2,1,0:T(8,128)S(1)}, u32[]{:S(2)}, u32[]{:S(2)}) collective-permute-start(f32[2,16,8,256]{3,2,1,0:T(8,128)S(1)} %get-tuple-element.38), channel_id=1, source_target_pairs={{0,4},{1,9},{2,6},{3,11},{4,0},{5,13},{6,2},{7,15},{8,12},{9,1},{1... | collective-permute-start | bytes 786440 | tf_op jit(solution)/shard_map/ppermute | solution.py:48
  19.6 0.3 collective-permute-done.14.refs_7_
  19.9 3.7 %shard_map.59 = (f32[2,16,8,256]{3,2,1,0:T(8,128)S(1)}, f32[2,16,8,256]{3,2,1,0:T(8,128)S(1)}) custom-call(s32[1,4]{1,0:T(1,128)S(1)} %copy-done.1, f32[4]{0:T(128)S(1)} %copy-done.2, f32[4]{0:T(128)S(1)} %copy-done.3, bf16[3,256,256]{2,1,0:T(8,128)(2,1)S(1)} %get-tuple-element.30.rate_high, bf16[3,256,256]{2,1,0:T(8,128)(2,1)S(1)} %get-tuple-element.31.rate_low, ...), custom_call_target="tpu_custom_call" | custom-call | tf_op jit(solution)/shard_map/pallas_call | solution.py:304
  23.6 1.6 %collective-permute-start.15 = (f32[2,16,8,256]{3,2,1,0:T(8,128)S(1)}, f32[2,16,8,256]{3,2,1,0:T(8,128)S(1)}, u32[]{:S(2)}, u32[]{:S(2)}) collective-permute-start(f32[2,16,8,256]{3,2,1,0:T(8,128)S(1)} %get-tuple-element.48), channel_id=1, source_target_pairs={{0,4},{1,9},{2,6},{3,11},{4,0},{5,13},{6,2},{7,15},{8,12},{9,1},{1... | collective-permute-start | bytes 786440 | tf_op jit(solution)/shard_map/ppermute | solution.py:48
  25.2 1.6 %collective-permute-start.4 = (f32[1,16,8,256]{3,2,1,0:T(8,128)S(1)}, f32[1,16,8,256]{3,2,1,0:T(8,128)S(1)}, u32[]{:S(2)}, u32[]{:S(2)}) collective-permute-start(f32[1,16,8,256]{3,2,1,0:T(8,128)S(1)} %slice.17), channel_id=1, source_target_pairs={{0,8},{1,5},{2,10},{3,7},{4,12},{5,1},{6,14},{7,3},{8,0},{9,13},{1... | collective-permute-start | bytes 393224 | tf_op jit(solution)/shard_map/ppermute | solution.py:48
  26.8 4.6 %collective-permute-done.15 = f32[2,16,8,256]{3,2,1,0:T(8,128)S(1)} collective-permute-done((f32[2,16,8,256]{3,2,1,0:T(8,128)S(1)}, f32[2,16,8,256]{3,2,1,0:T(8,128)S(1)}, u32[]{:S(2)}, u32[]{:S(2)}) %collective-permute-start.15) | collective-permute-done | bytes 262176 | tf_op jit(solution)/shard_map/ppermute | solution.py:48
  31.5 1.6 %collective-permute-start.16 = (f32[1,16,8,256]{3,2,1,0:T(8,128)S(1)}, f32[1,16,8,256]{3,2,1,0:T(8,128)S(1)}, u32[]{:S(2)}, u32[]{:S(2)}) collective-permute-start(f32[1,16,8,256]{3,2,1,0:T(8,128)S(1)} %slice.19), channel_id=1, source_target_pairs={{0,8},{1,5},{2,10},{3,7},{4,12},{5,1},{6,14},{7,3},{8,0},{9,13},{1... | collective-permute-start | bytes 393224 | tf_op jit(solution)/shard_map/ppermute | solution.py:48
  33.1 2.7 %collective-permute-start.5 = (f32[16,8,256]{2,1,0:T(8,128)S(1)}, f32[16,8,256]{2,1,0:T(8,128)S(1)}, u32[]{:S(2)}, u32[]{:S(2)}) collective-permute-start(f32[16,8,256]{2,1,0:T(8,128)S(1)} %fusion.1.refs_0_), channel_id=1, source_target_pairs={{0,16},{4,20},{8,24},{12,28},{16,0},{20,4},{24,8},{28,12},{1,17},{... | collective-permute-start | bytes 393224 | tf_op jit(solution)/shard_map/ppermute | solution.py:35
  35.7 2.1 %collective-permute-done.16 = f32[1,16,8,256]{3,2,1,0:T(8,128)S(1)} collective-permute-done((f32[1,16,8,256]{3,2,1,0:T(8,128)S(1)}, f32[1,16,8,256]{3,2,1,0:T(8,128)S(1)}, u32[]{:S(2)}, u32[]{:S(2)}) %collective-permute-start.16) | collective-permute-done | bytes 131104 | tf_op jit(solution)/shard_map/ppermute | solution.py:48
  37.9 2.7 %collective-permute-start.17 = (f32[16,8,256]{2,1,0:T(8,128)S(1)}, f32[16,8,256]{2,1,0:T(8,128)S(1)}, u32[]{:S(2)}, u32[]{:S(2)}) collective-permute-start(f32[16,8,256]{2,1,0:T(8,128)S(1)} %fusion.refs_0_), channel_id=1, source_target_pairs={{0,16},{4,20},{8,24},{12,28},{16,0},{20,4},{24,8},{28,12},{1,17},{... | collective-permute-start | bytes 393224 | tf_op jit(solution)/shard_map/ppermute | solution.py:35
  40.6 4.8 %collective-permute-done.5.refs_1_ = f32[16,8,256]{2,1,0:T(8,128)S(1)} collective-permute-done((f32[16,8,256]{2,1,0:T(8,128)S(1)}, f32[16,8,256]{2,1,0:T(8,128)S(1)}, u32[]{:S(2)}, u32[]{:S(2)}) %collective-permute-start.5) | collective-permute-done | bytes 131104 | tf_op jit(solution)/shard_map/ppermute | solution.py:35
  45.4 0.1 collective-permute-start.6
  45.5 1.6 %collective-permute-start.7 = (f32[1,5,8,256]{3,2,1,0:T(8,128)S(1)}, f32[1,5,8,256]{3,2,1,0:T(8,128)S(1)}, u32[]{:S(2)}, u32[]{:S(2)}) collective-permute-start(f32[1,5,8,256]{3,2,1,0:T(8,128)S(1)} %get-tuple-element.41), channel_id=1, source_target_pairs={{0,2},{1,3},{2,0},{3,1},{4,6},{5,7},{6,4},{7,5},{8,10},{9,11},{10,... | collective-permute-start | bytes 122888 | tf_op jit(solution)/shard_map/ppermute | solution.py:35
  47.1 0.2 collective-permute-start.8
  47.3 0.0 collective-permute-done.17.refs_1_
  47.3 0.4 collective-permute-start.18
  47.8 1.6 %collective-permute-start.22 = (f32[1,5,8,256]{3,2,1,0:T(8,128)S(1)}, f32[1,5,8,256]{3,2,1,0:T(8,128)S(1)}, u32[]{:S(2)}, u32[]{:S(2)}) collective-permute-start(f32[1,5,8,256]{3,2,1,0:T(8,128)S(1)} %get-tuple-element.51), channel_id=1, source_target_pairs={{0,2},{1,3},{2,0},{3,1},{4,6},{5,7},{6,4},{7,5},{8,10},{9,11},{10,... | collective-permute-start | bytes 122888 | tf_op jit(solution)/shard_map/ppermute | solution.py:35
  49.3 0.0 collective-permute-done.6
  49.3 0.2 collective-permute-done.7
  49.5 1.1 %collective-permute-done.8 = f32[1,5,8,256]{3,2,1,0:T(8,128)S(1)} collective-permute-done((f32[1,5,8,256]{3,2,1,0:T(8,128)S(1)}, f32[1,5,8,256]{3,2,1,0:T(8,128)S(1)}, u32[]{:S(2)}, u32[]{:S(2)}) %collective-permute-start.8) | collective-permute-done | bytes 40992 | tf_op jit(solution)/shard_map/ppermute | solution.py:35
  50.7 0.1 collective-permute-start.9
  50.7 1.1 %collective-permute-done.22 = f32[1,5,8,256]{3,2,1,0:T(8,128)S(1)} collective-permute-done((f32[1,5,8,256]{3,2,1,0:T(8,128)S(1)}, f32[1,5,8,256]{3,2,1,0:T(8,128)S(1)}, u32[]{:S(2)}, u32[]{:S(2)}) %collective-permute-start.22) | collective-permute-done | bytes 40992 | tf_op jit(solution)/shard_map/ppermute | solution.py:35
  51.8 1.3 %collective-permute-done.23 = f32[1,5,8,256]{3,2,1,0:T(8,128)S(1)} collective-permute-done((f32[1,5,8,256]{3,2,1,0:T(8,128)S(1)}, f32[1,5,8,256]{3,2,1,0:T(8,128)S(1)}, u32[]{:S(2)}, u32[]{:S(2)}) %collective-permute-start.23) | collective-permute-done | bytes 40992 | tf_op jit(solution)/shard_map/ppermute | solution.py:35
  53.2 0.3 collective-permute-start.24
  53.5 1.7 %collective-permute-start.10 = (f32[1,4,5,8,256]{4,3,2,1,0:T(8,128)S(1)}, f32[1,4,5,8,256]{4,3,2,1,0:T(8,128)S(1)}, u32[]{:S(2)}, u32[]{:S(2)}) collective-permute-start(f32[1,4,5,8,256]{4,3,2,1,0:T(8,128)S(1)} %maximum_bitcast_fusion.refs_0_), channel_id=1, source_target_pairs={{0,4},{1,9},{2,6},{3,11},{4,0},{5,13},{6,2},{7,15},{8,12},{9,1},{1... | collective-permute-start | bytes 491528 | tf_op jit(solution)/shard_map/ppermute | solution.py:48
  55.2 2.1 %collective-permute-start.19 = (f32[1,2,5,8,256]{4,3,2,1,0:T(8,128)S(1)}, f32[1,2,5,8,256]{4,3,2,1,0:T(8,128)S(1)}, u32[]{:S(2)}, u32[]{:S(2)}) collective-permute-start(f32[1,2,5,8,256]{4,3,2,1,0:T(8,128)S(1)} %maximum_bitcast_fusion.1.refs_4_), channel_id=1, source_target_pairs={{0,8},{1,5},{2,10},{3,7},{4,12},{5,1},{6,14},{7,3},{8,0},{9,13},{1... | collective-permute-start | bytes 245768 | tf_op jit(solution)/shard_map/ppermute | solution.py:48
  57.3 0.1 collective-permute-start.11
  57.4 0.6 collective-permute-done.25.refs_10_
  58.0 1.4 %collective-permute-start.20 = (f32[1,2,5,8,256]{4,3,2,1,0:T(8,128)S(1)}, f32[1,2,5,8,256]{4,3,2,1,0:T(8,128)S(1)}, u32[]{:S(2)}, u32[]{:S(2)}) collective-permute-start(f32[1,2,5,8,256]{4,3,2,1,0:T(8,128)S(1)} %maximum_bitcast_fusion.1.refs_4_), channel_id=1, source_target_pairs={{0,4},{1,9},{2,6},{3,11},{4,0},{5,13},{6,2},{7,15},{8,12},{9,1},{1... | collective-permute-start | bytes 245768 | tf_op jit(solution)/shard_map/ppermute | solution.py:48
  59.3 1.2 %collective-permute-start.26 = (f32[1,2,5,8,256]{4,3,2,1,0:T(8,128)S(1)}, f32[1,2,5,8,256]{4,3,2,1,0:T(8,128)S(1)}, u32[]{:S(2)}, u32[]{:S(2)}) collective-permute-start(f32[1,2,5,8,256]{4,3,2,1,0:T(8,128)S(1)} %collective-permute-done.24.refs_9_), channel_id=1, source_target_pairs={{0,4},{1,9},{2,6},{3,11},{4,0},{5,13},{6,2},{7,15},{8,12},{9,1},{1... | collective-permute-start | bytes 245768 | tf_op jit(solution)/shard_map/ppermute | solution.py:48
  60.5 0.1 collective-permute-done.19.refs_5_
  60.6 1.7 %collective-permute-start.21 = (f32[1,2,5,8,256]{4,3,2,1,0:T(8,128)S(1)}, f32[1,2,5,8,256]{4,3,2,1,0:T(8,128)S(1)}, u32[]{:S(2)}, u32[]{:S(2)}) collective-permute-start(f32[1,2,5,8,256]{4,3,2,1,0:T(8,128)S(1)} %collective-permute-done.19.refs_5_), channel_id=1, source_target_pairs={{0,4},{1,9},{2,6},{3,11},{4,0},{5,13},{6,2},{7,15},{8,12},{9,1},{1... | collective-permute-start | bytes 245768 | tf_op jit(solution)/shard_map/ppermute | solution.py:48
  62.3 1.2 %collective-permute-done.20.refs_6_ = f32[1,2,5,8,256]{4,3,2,1,0:T(8,128)S(1)} collective-permute-done((f32[1,2,5,8,256]{4,3,2,1,0:T(8,128)S(1)}, f32[1,2,5,8,256]{4,3,2,1,0:T(8,128)S(1)}, u32[]{:S(2)}, u32[]{:S(2)}) %collective-permute-start.20) | collective-permute-done | bytes 81952 | tf_op jit(solution)/shard_map/ppermute | solution.py:48
  63.5 0.9 %collective-permute-done.26.refs_11_ = f32[1,2,5,8,256]{4,3,2,1,0:T(8,128)S(1)} collective-permute-done((f32[1,2,5,8,256]{4,3,2,1,0:T(8,128)S(1)}, f32[1,2,5,8,256]{4,3,2,1,0:T(8,128)S(1)}, u32[]{:S(2)}, u32[]{:S(2)}) %collective-permute-start.26) | collective-permute-done | bytes 81952 | tf_op jit(solution)/shard_map/ppermute | solution.py:48
  64.4 0.9 %collective-permute-done.21.refs_7_ = f32[1,2,5,8,256]{4,3,2,1,0:T(8,128)S(1)} collective-permute-done((f32[1,2,5,8,256]{4,3,2,1,0:T(8,128)S(1)}, f32[1,2,5,8,256]{4,3,2,1,0:T(8,128)S(1)}, u32[]{:S(2)}, u32[]{:S(2)}) %collective-permute-start.21) | collective-permute-done | bytes 81952 | tf_op jit(solution)/shard_map/ppermute | solution.py:48
  65.3 2.4 %shard_map.61 = f32[4,256,256]{2,1,0:T(8,128)} custom-call(s32[1,4]{1,0:T(1,128)S(1)} %copy-done.1, bf16[256,256]{1,0:T(8,128)(2,1)S(1)} %get-tuple-element.29.lane_restore, f32[1,4,5,8,256]{4,3,2,1,0:T(8,128)S(1)} %maximum_bitcast_fusion.refs_0_, f32[1,4,5,8,256]{4,3,2,1,0:T(8,128)S(1)} %collective-permute-done.9.refs_1_, ...), custom_call_target="tpu_custom_call" | custom-call | tf_op jit(solution)/shard_map/pallas_call | solution.py:410
  (30 shorter events, 0.2 us)
Async XLA Ops:
  0.0 1.2 %copy-start = (f32[1,4,16,16,256]{4,3,2,1,0:T(8,128)S(1)}, f32[1,4,16,16,256]{4,3,2,1,0:T(8,128)}, u32[]{:S(2)}) copy-start(f32[1,4,16,16,256]{4,3,2,1,0:T(8,128)} %param.5) | copy-start | bytes 3145732
  1.7 7.6 %collective-permute-start = (f32[4,48,256]{2,1,0:T(8,128)S(1)}, f32[4,48,256]{2,1,0:T(8,128)S(1)}, u32[]{:S(2)}, u32[]{:S(2)}) collective-permute-start(f32[4,48,256]{2,1,0:T(8,128)S(1)} %get-tuple-element.34), channel_id=1, source_target_pairs={{0,1},{1,0},{2,3},{3,2},{4,5},{5,4},{6,7},{7,6},{8,9},{9,8},{10,11... | collective-permute-start | bytes 589832 | tf_op jit(solution)/shard_map/ppermute | solution.py:35
  2.3 8.3 %collective-permute-start.1 = (f32[4,48,256]{2,1,0:T(8,128)S(1)}, f32[4,48,256]{2,1,0:T(8,128)S(1)}, u32[]{:S(2)}, u32[]{:S(2)}) collective-permute-start(f32[4,48,256]{2,1,0:T(8,128)S(1)} %get-tuple-element.35), channel_id=1, source_target_pairs={{0,2},{1,3},{2,0},{3,1},{4,6},{5,7},{6,4},{7,5},{8,10},{9,11},{10,... | collective-permute-start | bytes 589832 | tf_op jit(solution)/shard_map/ppermute | solution.py:35
  4.8 9.5 %collective-permute-start.2 = (f32[4,48,256]{2,1,0:T(8,128)S(1)}, f32[4,48,256]{2,1,0:T(8,128)S(1)}, u32[]{:S(2)}, u32[]{:S(2)}) collective-permute-start(f32[4,48,256]{2,1,0:T(8,128)S(1)} %get-tuple-element.36), channel_id=1, source_target_pairs={{0,3},{1,2},{2,1},{3,0},{4,7},{5,6},{6,5},{7,4},{8,11},{9,10},{10,... | collective-permute-start | bytes 589832 | tf_op jit(solution)/shard_map/ppermute | solution.py:35
  4.8 14.8 %collective-permute-start.12 = (f32[4,32,256]{2,1,0:T(8,128)S(1)}, f32[4,32,256]{2,1,0:T(8,128)S(1)}, u32[]{:S(2)}, u32[]{:S(2)}) collective-permute-start(f32[4,32,256]{2,1,0:T(8,128)S(1)} %get-tuple-element.44), channel_id=1, source_target_pairs={{0,1},{1,0},{2,3},{3,2},{4,5},{5,4},{6,7},{7,6},{8,9},{9,8},{10,11... | collective-permute-start | bytes 393224 | tf_op jit(solution)/shard_map/ppermute | solution.py:35
  5.0 2.6 %copy-start.1 = (s32[1,4]{1,0:T(1,128)S(1)}, s32[1,4]{1,0:T(1,128)}, u32[]{:S(2)}) copy-start(s32[1,4]{1,0:T(1,128)} %cut_ref.7) | copy-start | bytes 52
  5.0 2.6 %copy-start.2 = (f32[4]{0:T(128)S(1)}, f32[4]{0:T(128)}, u32[]{:S(2)}) copy-start(f32[4]{0:T(128)} %diff_ref.5) | copy-start | bytes 52
  5.0 2.6 %copy-start.3 = (f32[4]{0:T(128)S(1)}, f32[4]{0:T(128)}, u32[]{:S(2)}) copy-start(f32[4]{0:T(128)} %cour_ref.5) | copy-start | bytes 52
  5.0 14.6 %collective-permute-start.13 = (f32[4,32,256]{2,1,0:T(8,128)S(1)}, f32[4,32,256]{2,1,0:T(8,128)S(1)}, u32[]{:S(2)}, u32[]{:S(2)}) collective-permute-start(f32[4,32,256]{2,1,0:T(8,128)S(1)} %get-tuple-element.45), channel_id=1, source_target_pairs={{0,2},{1,3},{2,0},{3,1},{4,6},{5,7},{6,4},{7,5},{8,10},{9,11},{10,... | collective-permute-start | bytes 393224 | tf_op jit(solution)/shard_map/ppermute | solution.py:35
  9.3 10.5 %collective-permute-start.14 = (f32[4,32,256]{2,1,0:T(8,128)S(1)}, f32[4,32,256]{2,1,0:T(8,128)S(1)}, u32[]{:S(2)}, u32[]{:S(2)}) collective-permute-start(f32[4,32,256]{2,1,0:T(8,128)S(1)} %get-tuple-element.46), channel_id=1, source_target_pairs={{0,3},{1,2},{2,1},{3,0},{4,7},{5,6},{6,5},{7,4},{8,11},{9,10},{10,... | collective-permute-start | bytes 393224 | tf_op jit(solution)/shard_map/ppermute | solution.py:35
  18.0 7.1 %collective-permute-start.3 = (f32[2,16,8,256]{3,2,1,0:T(8,128)S(1)}, f32[2,16,8,256]{3,2,1,0:T(8,128)S(1)}, u32[]{:S(2)}, u32[]{:S(2)}) collective-permute-start(f32[2,16,8,256]{3,2,1,0:T(8,128)S(1)} %get-tuple-element.38), channel_id=1, source_target_pairs={{0,4},{1,9},{2,6},{3,11},{4,0},{5,13},{6,2},{7,15},{8,12},{9,1},{1... | collective-permute-start | bytes 786440 | tf_op jit(solution)/shard_map/ppermute | solution.py:48
  23.6 7.8 %collective-permute-start.15 = (f32[2,16,8,256]{3,2,1,0:T(8,128)S(1)}, f32[2,16,8,256]{3,2,1,0:T(8,128)S(1)}, u32[]{:S(2)}, u32[]{:S(2)}) collective-permute-start(f32[2,16,8,256]{3,2,1,0:T(8,128)S(1)} %get-tuple-element.48), channel_id=1, source_target_pairs={{0,4},{1,9},{2,6},{3,11},{4,0},{5,13},{6,2},{7,15},{8,12},{9,1},{1... | collective-permute-start | bytes 786440 | tf_op jit(solution)/shard_map/ppermute | solution.py:48
  25.2 7.9 %collective-permute-start.4 = (f32[1,16,8,256]{3,2,1,0:T(8,128)S(1)}, f32[1,16,8,256]{3,2,1,0:T(8,128)S(1)}, u32[]{:S(2)}, u32[]{:S(2)}) collective-permute-start(f32[1,16,8,256]{3,2,1,0:T(8,128)S(1)} %slice.17), channel_id=1, source_target_pairs={{0,8},{1,5},{2,10},{3,7},{4,12},{5,1},{6,14},{7,3},{8,0},{9,13},{1... | collective-permute-start | bytes 393224 | tf_op jit(solution)/shard_map/ppermute | solution.py:48
  31.5 6.4 %collective-permute-start.16 = (f32[1,16,8,256]{3,2,1,0:T(8,128)S(1)}, f32[1,16,8,256]{3,2,1,0:T(8,128)S(1)}, u32[]{:S(2)}, u32[]{:S(2)}) collective-permute-start(f32[1,16,8,256]{3,2,1,0:T(8,128)S(1)} %slice.19), channel_id=1, source_target_pairs={{0,8},{1,5},{2,10},{3,7},{4,12},{5,1},{6,14},{7,3},{8,0},{9,13},{1... | collective-permute-start | bytes 393224 | tf_op jit(solution)/shard_map/ppermute | solution.py:48
  33.1 12.3 %collective-permute-start.5 = (f32[16,8,256]{2,1,0:T(8,128)S(1)}, f32[16,8,256]{2,1,0:T(8,128)S(1)}, u32[]{:S(2)}, u32[]{:S(2)}) collective-permute-start(f32[16,8,256]{2,1,0:T(8,128)S(1)} %fusion.1.refs_0_), channel_id=1, source_target_pairs={{0,16},{4,20},{8,24},{12,28},{16,0},{20,4},{24,8},{28,12},{1,17},{... | collective-permute-start | bytes 393224 | tf_op jit(solution)/shard_map/ppermute | solution.py:35
  37.9 9.5 %collective-permute-start.17 = (f32[16,8,256]{2,1,0:T(8,128)S(1)}, f32[16,8,256]{2,1,0:T(8,128)S(1)}, u32[]{:S(2)}, u32[]{:S(2)}) collective-permute-start(f32[16,8,256]{2,1,0:T(8,128)S(1)} %fusion.refs_0_), channel_id=1, source_target_pairs={{0,16},{4,20},{8,24},{12,28},{16,0},{20,4},{24,8},{28,12},{1,17},{... | collective-permute-start | bytes 393224 | tf_op jit(solution)/shard_map/ppermute | solution.py:35
  45.4 4.0 %collective-permute-start.6 = (f32[1,5,8,256]{3,2,1,0:T(8,128)S(1)}, f32[1,5,8,256]{3,2,1,0:T(8,128)S(1)}, u32[]{:S(2)}, u32[]{:S(2)}) collective-permute-start(f32[1,5,8,256]{3,2,1,0:T(8,128)S(1)} %get-tuple-element.40), channel_id=1, source_target_pairs={{0,1},{1,0},{2,3},{3,2},{4,5},{5,4},{6,7},{7,6},{8,9},{9,8},{10,11... | collective-permute-start | bytes 122888 | tf_op jit(solution)/shard_map/ppermute | solution.py:35
  45.5 4.1 %collective-permute-start.7 = (f32[1,5,8,256]{3,2,1,0:T(8,128)S(1)}, f32[1,5,8,256]{3,2,1,0:T(8,128)S(1)}, u32[]{:S(2)}, u32[]{:S(2)}) collective-permute-start(f32[1,5,8,256]{3,2,1,0:T(8,128)S(1)} %get-tuple-element.41), channel_id=1, source_target_pairs={{0,2},{1,3},{2,0},{3,1},{4,6},{5,7},{6,4},{7,5},{8,10},{9,11},{10,... | collective-permute-start | bytes 122888 | tf_op jit(solution)/shard_map/ppermute | solution.py:35
  47.1 3.5 %collective-permute-start.8 = (f32[1,5,8,256]{3,2,1,0:T(8,128)S(1)}, f32[1,5,8,256]{3,2,1,0:T(8,128)S(1)}, u32[]{:S(2)}, u32[]{:S(2)}) collective-permute-start(f32[1,5,8,256]{3,2,1,0:T(8,128)S(1)} %get-tuple-element.42), channel_id=1, source_target_pairs={{0,3},{1,2},{2,1},{3,0},{4,7},{5,6},{6,5},{7,4},{8,11},{9,10},{10,... | collective-permute-start | bytes 122888 | tf_op jit(solution)/shard_map/ppermute | solution.py:35
  47.3 7.8 %collective-permute-start.18 = (f32[1,5,8,256]{3,2,1,0:T(8,128)S(1)}, f32[1,5,8,256]{3,2,1,0:T(8,128)S(1)}, u32[]{:S(2)}, u32[]{:S(2)}) collective-permute-start(f32[1,5,8,256]{3,2,1,0:T(8,128)S(1)} %get-tuple-element.50), channel_id=1, source_target_pairs={{0,1},{1,0},{2,3},{3,2},{4,5},{5,4},{6,7},{7,6},{8,9},{9,8},{10,11... | collective-permute-start | bytes 122888 | tf_op jit(solution)/shard_map/ppermute | solution.py:35
  47.8 4.1 %collective-permute-start.22 = (f32[1,5,8,256]{3,2,1,0:T(8,128)S(1)}, f32[1,5,8,256]{3,2,1,0:T(8,128)S(1)}, u32[]{:S(2)}, u32[]{:S(2)}) collective-permute-start(f32[1,5,8,256]{3,2,1,0:T(8,128)S(1)} %get-tuple-element.51), channel_id=1, source_target_pairs={{0,2},{1,3},{2,0},{3,1},{4,6},{5,7},{6,4},{7,5},{8,10},{9,11},{10,... | collective-permute-start | bytes 122888 | tf_op jit(solution)/shard_map/ppermute | solution.py:35
  49.3 3.8 %collective-permute-start.23 = (f32[1,5,8,256]{3,2,1,0:T(8,128)S(1)}, f32[1,5,8,256]{3,2,1,0:T(8,128)S(1)}, u32[]{:S(2)}, u32[]{:S(2)}) collective-permute-start(f32[1,5,8,256]{3,2,1,0:T(8,128)S(1)} %get-tuple-element.52), channel_id=1, source_target_pairs={{0,3},{1,2},{2,1},{3,0},{4,7},{5,6},{6,5},{7,4},{8,11},{9,10},{10,... | collective-permute-start | bytes 122888 | tf_op jit(solution)/shard_map/ppermute | solution.py:35
  50.7 6.6 %collective-permute-start.9 = (f32[1,4,5,8,256]{4,3,2,1,0:T(8,128)S(1)}, f32[1,4,5,8,256]{4,3,2,1,0:T(8,128)S(1)}, u32[]{:S(2)}, u32[]{:S(2)}) collective-permute-start(f32[1,4,5,8,256]{4,3,2,1,0:T(8,128)S(1)} %maximum_bitcast_fusion.refs_0_), channel_id=1, source_target_pairs={{0,8},{1,5},{2,10},{3,7},{4,12},{5,1},{6,14},{7,3},{8,0},{9,13},{1... | collective-permute-start | bytes 491528 | tf_op jit(solution)/shard_map/ppermute | solution.py:48
  53.2 4.8 %collective-permute-start.25 = (f32[1,2,5,8,256]{4,3,2,1,0:T(8,128)S(1)}, f32[1,2,5,8,256]{4,3,2,1,0:T(8,128)S(1)}, u32[]{:S(2)}, u32[]{:S(2)}) collective-permute-start(f32[1,2,5,8,256]{4,3,2,1,0:T(8,128)S(1)} %maximum_bitcast_fusion.2.refs_8_), channel_id=1, source_target_pairs={{0,4},{1,9},{2,6},{3,11},{4,0},{5,13},{6,2},{7,15},{8,12},{9,1},{1... | collective-permute-start | bytes 245768 | tf_op jit(solution)/shard_map/ppermute | solution.py:48
  53.2 6.2 %collective-permute-start.24 = (f32[1,2,5,8,256]{4,3,2,1,0:T(8,128)S(1)}, f32[1,2,5,8,256]{4,3,2,1,0:T(8,128)S(1)}, u32[]{:S(2)}, u32[]{:S(2)}) collective-permute-start(f32[1,2,5,8,256]{4,3,2,1,0:T(8,128)S(1)} %maximum_bitcast_fusion.2.refs_8_), channel_id=1, source_target_pairs={{0,8},{1,5},{2,10},{3,7},{4,12},{5,1},{6,14},{7,3},{8,0},{9,13},{1... | collective-permute-start | bytes 245768 | tf_op jit(solution)/shard_map/ppermute | solution.py:48
  53.5 10.0 %collective-permute-start.10 = (f32[1,4,5,8,256]{4,3,2,1,0:T(8,128)S(1)}, f32[1,4,5,8,256]{4,3,2,1,0:T(8,128)S(1)}, u32[]{:S(2)}, u32[]{:S(2)}) collective-permute-start(f32[1,4,5,8,256]{4,3,2,1,0:T(8,128)S(1)} %maximum_bitcast_fusion.refs_0_), channel_id=1, source_target_pairs={{0,4},{1,9},{2,6},{3,11},{4,0},{5,13},{6,2},{7,15},{8,12},{9,1},{1... | collective-permute-start | bytes 491528 | tf_op jit(solution)/shard_map/ppermute | solution.py:48
  55.2 5.4 %collective-permute-start.19 = (f32[1,2,5,8,256]{4,3,2,1,0:T(8,128)S(1)}, f32[1,2,5,8,256]{4,3,2,1,0:T(8,128)S(1)}, u32[]{:S(2)}, u32[]{:S(2)}) collective-permute-start(f32[1,2,5,8,256]{4,3,2,1,0:T(8,128)S(1)} %maximum_bitcast_fusion.1.refs_4_), channel_id=1, source_target_pairs={{0,8},{1,5},{2,10},{3,7},{4,12},{5,1},{6,14},{7,3},{8,0},{9,13},{1... | collective-permute-start | bytes 245768 | tf_op jit(solution)/shard_map/ppermute | solution.py:48
  57.3 8.0 %collective-permute-start.11 = (f32[1,4,5,8,256]{4,3,2,1,0:T(8,128)S(1)}, f32[1,4,5,8,256]{4,3,2,1,0:T(8,128)S(1)}, u32[]{:S(2)}, u32[]{:S(2)}) collective-permute-start(f32[1,4,5,8,256]{4,3,2,1,0:T(8,128)S(1)} %collective-permute-done.9.refs_1_), channel_id=1, source_target_pairs={{0,4},{1,9},{2,6},{3,11},{4,0},{5,13},{6,2},{7,15},{8,12},{9,1},{1... | collective-permute-start | bytes 491528 | tf_op jit(solution)/shard_map/ppermute | solution.py:48
  58.0 5.5 %collective-permute-start.20 = (f32[1,2,5,8,256]{4,3,2,1,0:T(8,128)S(1)}, f32[1,2,5,8,256]{4,3,2,1,0:T(8,128)S(1)}, u32[]{:S(2)}, u32[]{:S(2)}) collective-permute-start(f32[1,2,5,8,256]{4,3,2,1,0:T(8,128)S(1)} %maximum_bitcast_fusion.1.refs_4_), channel_id=1, source_target_pairs={{0,4},{1,9},{2,6},{3,11},{4,0},{5,13},{6,2},{7,15},{8,12},{9,1},{1... | collective-permute-start | bytes 245768 | tf_op jit(solution)/shard_map/ppermute | solution.py:48
  59.3 5.0 %collective-permute-start.26 = (f32[1,2,5,8,256]{4,3,2,1,0:T(8,128)S(1)}, f32[1,2,5,8,256]{4,3,2,1,0:T(8,128)S(1)}, u32[]{:S(2)}, u32[]{:S(2)}) collective-permute-start(f32[1,2,5,8,256]{4,3,2,1,0:T(8,128)S(1)} %collective-permute-done.24.refs_9_), channel_id=1, source_target_pairs={{0,4},{1,9},{2,6},{3,11},{4,0},{5,13},{6,2},{7,15},{8,12},{9,1},{1... | collective-permute-start | bytes 245768 | tf_op jit(solution)/shard_map/ppermute | solution.py:48
  60.6 4.7 %collective-permute-start.21 = (f32[1,2,5,8,256]{4,3,2,1,0:T(8,128)S(1)}, f32[1,2,5,8,256]{4,3,2,1,0:T(8,128)S(1)}, u32[]{:S(2)}, u32[]{:S(2)}) collective-permute-start(f32[1,2,5,8,256]{4,3,2,1,0:T(8,128)S(1)} %collective-permute-done.19.refs_5_), channel_id=1, source_target_pairs={{0,4},{1,9},{2,6},{3,11},{4,0},{5,13},{6,2},{7,15},{8,12},{9,1},{1... | collective-permute-start | bytes 245768 | tf_op jit(solution)/shard_map/ppermute | solution.py:48
